TPU v7x, 512 devices: a whole 4x8x8 slice. The times are simulated.
512 devices in a mesh: narrow: 8 (over z), wide: 64 (over x, y, core).
Axes of the slice: x: 4, y: 8, z: 8, core: 2. Of those that a mesh axis runs over, the one named last changes fastest.
Arguments:
- momentum: float32 [4096, 28672], P('narrow', 'wide'), may hold values from -16 to 16
- gradient: bfloat16 [4096, 28672], P('narrow', 'wide'), may hold values from -6 to 6
- right_basis: float32 [28672, 256], P('wide'), may hold values from -0.03125 to 0.03125
- signs: int32 [4096], replicated, may hold values from -1 to 1, as said below
- select: int32 [384], replicated, may hold values from 0 to 4095, as said below
Outputs:
- momentum_out: float32 [4096, 28672], P('narrow', 'wide')
- basis_out: float32 [28672, 256], P('wide')
- update: bfloat16 [4096, 28672], P('narrow', 'wide')
Inputs may be any that keep to these rules, and one draw needn't show every extreme that they name: `signs`: each entry is -1 or 1. `select`: 384 distinct row numbers.
All inputs are finite; a program needn't handle non-finite values.
Results may differ from a plain program's by a relative error of at most 0.001.
Values sent between devices are 32-bit elements; how exact they have to be, the bound alone decides.
A program may use at most 64 MiB of HBM per device.

v0:
```python
import math

import jax
import jax.numpy as jnp
from jax import lax
from jax.sharding import Mesh
from jax.sharding import PartitionSpec as P

ROWS = 4096
COLS = 28672
RANK = 256
SKETCH = 384
WIDE = ("wide_0", "wide_1", "wide_2")


decay_mu = 0.95
norm_epsilon = 1e-06


def cut_along(value, dim, devices):
    shape = value.shape
    parts = value.reshape(*shape[:dim], devices, shape[dim] // devices, *shape[dim + 1 :])
    return jnp.moveaxis(parts, dim, 0)


def summed_on_arrival(value, axis, dim):
    devices = lax.axis_size(axis)
    parts = lax.all_to_all(cut_along(value, dim, devices), axis, 0, 0, tiled=True)
    return jnp.sum(parts, axis=0)


def rows_for(lines, devices):
    spare = -lines.shape[0] % devices
    if not spare:
        return lines
    return jnp.concatenate([lines, jnp.zeros((spare, *lines.shape[1:]), lines.dtype)])


def sent_to_all(value, axis):
    devices = lax.axis_size(axis)
    return lax.all_to_all(
        jnp.broadcast_to(value[None], (devices, *value.shape)), axis, 0, 0, tiled=True
    )


def in_order(parts, dim):
    shape = list(parts.shape[1:])
    shape[dim] *= parts.shape[0]
    return jnp.moveaxis(parts, 0, dim).reshape(shape)


def gather_directly(value, axis, dim):
    parts = sent_to_all(value, axis)
    return in_order(parts, dim)


def nested_sum(value, axes):
    lines = value.reshape(-1, value.shape[-1])
    own = summed_on_arrival(rows_for(lines, lax.axis_size(axes)), axes, 0)
    whole = gather_directly(own, axes, 0)
    return whole[: len(lines)].reshape(value.shape)


def taken_together(value, axis):
    everything = sent_to_all(value, axis)
    return jnp.sum(everything, axis=0)


def one_axis_at_a_time(value, axes):
    far, near = axes
    nearer = taken_together(value, near)
    return taken_together(nearer, far)


def hadamard_rows(select, sign_part, first_row, row_count):
    columns = first_row + jnp.arange(row_count, dtype=jnp.int32)
    shared_bits = jnp.bitwise_and(select[:, None], columns[None, :])
    parity = jnp.zeros(shared_bits.shape, jnp.int32)
    for bit_index in range(ROWS.bit_length()):
        parity = jnp.bitwise_xor(
            parity, jnp.bitwise_and(jnp.right_shift(shared_bits, bit_index), 1)
        )
    entries = (1 - 2 * parity).astype(jnp.float32) * sign_part.astype(jnp.float32)[None, :]
    return entries / math.sqrt(SKETCH)


def sketch_term(select, signs, first_row, row_values):
    row_count = row_values.shape[0]
    sign_part = lax.dynamic_slice_in_dim(signs, first_row, row_count)
    hadamard = hadamard_rows(select, sign_part, first_row, row_count)
    return jnp.dot(
        hadamard, row_values, precision=lax.Precision.HIGHEST, preferred_element_type=jnp.float32
    )


def orthonormal(sketch, row_values):
    gram = jnp.dot(
        sketch.T, sketch, precision=lax.Precision.HIGHEST, preferred_element_type=jnp.float32
    )
    lower_factor = jnp.linalg.cholesky(gram)
    return jax.scipy.linalg.solve_triangular(lower_factor, row_values.T, lower=True).T


def per_device(momentum, gradient, right_basis, signs, select):
    high = lax.Precision.HIGHEST
    summed = momentum + gradient.astype(jnp.float32)
    block_rows = summed.shape[0]
    narrow_index = lax.axis_index("narrow")
    block_start = narrow_index * block_rows
    partial_left = jnp.dot(summed, right_basis, precision=high, preferred_element_type=jnp.float32)
    row_block = nested_sum(partial_left, WIDE)
    sketch = taken_together(sketch_term(select, signs, block_start, row_block), "narrow")
    left_full = orthonormal(sketch, row_block)
    right_share = summed_on_arrival(
        lax.dot_general(
            summed,
            left_full,
            (((0,), (0,)), ((), ())),
            precision=high,
            preferred_element_type=jnp.float32,
        ),
        "narrow",
        0,
    )
    squares = jnp.sum(right_share * right_share, axis=0)
    norms = jnp.sqrt(
        one_axis_at_a_time(squares, ("narrow", ("wide_0", "wide_1", "wide_2"))) + norm_epsilon
    )
    normalized = right_share / norms[None, :]
    basis_out = gather_directly(normalized, "narrow", 0)
    right_full = basis_out * norms[None, :]
    momentum_out = summed - (1.0 - decay_mu) * jnp.dot(
        left_full, right_full.T, precision=high, preferred_element_type=jnp.float32
    )
    scale_factor = math.sqrt(ROWS * COLS / RANK)
    update = (
        scale_factor
        * jnp.dot(left_full, basis_out.T, precision=high, preferred_element_type=jnp.float32)
    ).astype(jnp.bfloat16)
    return (momentum_out, basis_out, update)


def solution(mesh):
    split = Mesh(
        mesh.devices.reshape(mesh.shape["narrow"], 4, 8, 2),
        ("narrow", "wide_0", "wide_1", "wide_2"),
    )
    in_specs = (P("narrow", WIDE), P("narrow", WIDE), P(WIDE, None), P(), P())
    out_specs = (P("narrow", WIDE), P(WIDE, None), P("narrow", WIDE))
    return jax.shard_map(
        per_device, mesh=split, in_specs=in_specs, out_specs=out_specs, check_vma=False
    )
```

profile of v0, /device:TPU:1, one launch (start us, length us, event | category | flops | bytes accessed | tf_op | source)
XLA Modules:
  0.0 276.7 jit_solution(374259006938859194)
XLA Ops:
  0.6 1.0 copy-done
  1.7 3.1 %convolution_bitcast_fusion = f32[64,8,256]{2,1,0:T(8,128)S(1)} fusion(f32[448,256]{1,0:T(8,128)S(1)} %copy-done, f32[512,448]{0,1:T(8,128)} %param.5, bf16[512,448]{0,1:T(8,128)(2,1)} %param.6), kind=kOutput, calls=%fused_computation.19 | convolution fusion | flops 705101824 | bytes 2359296 | tf_op jit(solution)/shard_map/dot_general | solution.py:110
  4.8 28.7 %all_to_all.37 = f32[64,8,256]{2,1,0:T(8,128)S(1)} all-to-all(f32[64,8,256]{2,1,0:T(8,128)S(1)} %convolution_bitcast_fusion), channel_id=1, replica_groups=mesh['narrow'=8,'wide_0'=4,'wide_1'=8,'wide_2'=2] {'wide_0','wide_1','wi..., dimensions={0} | all-to-all | bytes 1048576 | tf_op jit(solution)/shard_map/all_to_all | solution.py:28
  34.4 6.3 %all-to-all-start.1 = ((f32[64,8,256]{2,1,0:T(8,128)}), f32[64,8,256]{2,1,0:T(8,128)S(1)}, u32[]{:S(2)}, u32[]{:S(2)}) async-start(f32[64,8,256]{2,1,0:T(8,128)} %broadcast_in_dim.11), calls=%async_computation.1 | async-start | bytes 1048576 | tf_op jit(solution)/shard_map/all_to_all | solution.py:41
  41.5 16.5 %all-to-all-done.1 = f32[64,8,256]{2,1,0:T(8,128)S(1)} async-done(((f32[64,8,256]{2,1,0:T(8,128)}), f32[64,8,256]{2,1,0:T(8,128)S(1)}, u32[]{:S(2)}, u32[]{:S(2)}) %all-to-all-start.1) | async-done | bytes 524320 | tf_op jit(solution)/shard_map/all_to_all | solution.py:41
  58.0 1.9 fusion.32
  59.9 2.0 broadcast_in_dim.13
  61.9 10.0 %all-to-all-start.2 = ((f32[8,384,256]{2,1,0:T(8,128)}), f32[8,384,256]{2,1,0:T(8,128)}, u32[]{:S(2)}, u32[]{:S(2)}) async-start(f32[8,384,256]{2,1,0:T(8,128)} %broadcast_in_dim.13), calls=%async_computation.2 | async-start | bytes 6291456 | tf_op jit(solution)/shard_map/all_to_all | solution.py:41
  72.1 74.1 %all-to-all-done.2 = f32[8,384,256]{2,1,0:T(8,128)} async-done(((f32[8,384,256]{2,1,0:T(8,128)}), f32[8,384,256]{2,1,0:T(8,128)}, u32[]{:S(2)}, u32[]{:S(2)}) %all-to-all-start.2) | async-done | bytes 3145760 | tf_op jit(solution)/shard_map/all_to_all | solution.py:41
  146.2 2.1 reduce_sum.55
  149.4 11.7 %cholesky.50 = f32[128,128]{1,0:T(8,128)S(1)} custom-call(f32[128,128]{1,0:T(8,128)S(1)} %cholesky.118), custom_call_target="Cholesky" | custom-call | tf_op jit(solution)/shard_map/jit(cholesky)/cholesky | solution.py:100
  161.1 9.8 %custom-call.15 = f32[1,128,128]{1,2,0:T(8,128)S(1)} custom-call(f32[1,128,128]{2,1,0:T(8,128)S(1)} %get-tuple-element.24), custom_call_target="InvertDiagBlocksLowerTriangular" | custom-call | tf_op jit(solution)/shard_map/jit(cholesky)/cholesky | solution.py:100
  171.4 11.7 %cholesky.105 = f32[128,128]{1,0:T(8,128)S(1)} custom-call(f32[128,128]{1,0:T(8,128)S(1)} %convolution_subtract_fusion.1), custom_call_target="Cholesky" | custom-call | tf_op jit(solution)/shard_map/jit(cholesky)/cholesky | solution.py:100
  185.9 4.0 %while.1 = (s32[]{:T(128)}, f32[256,256]{1,0:T(8,128)S(1)}, s32[2,2]{1,0:T(2,128)S(1)}, f32[2,128,128]{2,1,0:T(8,128)S(1)}, s32[]{:T(128)}) while((s32[]{:T(128)}, f32[256,256]{1,0:T(8,128)S(1)}, s32[2,2]{1,0:T(2,128)S(1)}, f32[2,128,128]{2,1,0:T(8,128)S(1)}, s32[]{:T(128)}) %tuple.27), condition=%wide.while_cond, body=%wide.while_body.sunk | while | flops 2 | bytes 131181 | solution.py:101
  186.5 1.4 bitcast_dynamic-update-slice_fusion.2
  188.5 1.4 bitcast_dynamic-update-slice_fusion.2
  189.9 19.9 %custom-call.16 = f32[2,128,128]{1,2,0:T(8,128)S(1)} custom-call(f32[2,128,128]{2,1,0:T(8,128)S(1)} %get-tuple-element.10), custom_call_target="InvertDiagBlocksLowerTriangular" | custom-call | tf_op jit(solution)/shard_map/jit(_solve_triangular)/triangular_solve | solution.py:101
  211.0 0.9 fusion.52
  212.0 18.8 %all_to_all.38 = f32[8,56,256]{2,1,0:T(8,128)S(1)} all-to-all(f32[8,56,256]{2,1,0:T(8,128)S(1)} %bitcast.49), channel_id=1, replica_groups=mesh['narrow'=8,'wide_0'=4,'wide_1'=8,'wide_2'=2] {'narrow'}, dimensions={0} | all-to-all | bytes 917504 | tf_op jit(solution)/shard_map/all_to_all | solution.py:28
  230.9 15.8 %all_to_all.39 = f32[64,1,256]{2,1,0:T(1,128)S(1)} all-to-all(f32[64,1,256]{2,1,0:T(1,128)S(1)} %broadcast_in_dim.14), channel_id=1, replica_groups=mesh['narrow'=8,'wide_0'=4,'wide_1'=8,'wide_2'=2] {'wide_0','wide_1','wi..., dimensions={0} | all-to-all | bytes 131072 | tf_op jit(solution)/shard_map/all_to_all | solution.py:41
  246.8 8.9 %all_to_all.40 = f32[8,1,256]{2,1,0:T(1,128)S(1)} all-to-all(f32[8,1,256]{2,1,0:T(1,128)S(1)} %broadcast_in_dim.15), channel_id=1, replica_groups=mesh['narrow'=8,'wide_0'=4,'wide_1'=8,'wide_2'=2] {'narrow'}, dimensions={0} | all-to-all | bytes 16384 | tf_op jit(solution)/shard_map/all_to_all | solution.py:41
  255.8 16.5 %all_to_all.41 = f32[8,56,256]{2,1,0:T(8,128)S(1)} all-to-all(f32[8,56,256]{2,1,0:T(8,128)S(1)} %broadcast_in_dim.16), channel_id=1, replica_groups=mesh['narrow'=8,'wide_0'=4,'wide_1'=8,'wide_2'=2] {'narrow'}, dimensions={0} | all-to-all | bytes 917504 | tf_op jit(solution)/shard_map/all_to_all | solution.py:41
  272.3 1.7 fusion.1
  274.0 1.9 fusion
  (43 shorter events, 8.3 us)
Async XLA Ops:
  0.6 1.0 copy-start
  1.7 56.3 %copy-start.3 = (s32[384]{0:T(512)S(1)}, s32[384]{0:T(512)}, u32[]{:S(2)}) copy-start(s32[384]{0:T(512)} %param.9) | copy-start | bytes 4612
  34.4 23.6 %all-to-all-start.1 = ((f32[64,8,256]{2,1,0:T(8,128)}), f32[64,8,256]{2,1,0:T(8,128)S(1)}, u32[]{:S(2)}, u32[]{:S(2)}) async-start(f32[64,8,256]{2,1,0:T(8,128)} %broadcast_in_dim.11), calls=%async_computation.1 | async-start | bytes 1048576 | tf_op jit(solution)/shard_map/all_to_all | solution.py:41
  61.9 84.3 %all-to-all-start.2 = ((f32[8,384,256]{2,1,0:T(8,128)}), f32[8,384,256]{2,1,0:T(8,128)}, u32[]{:S(2)}, u32[]{:S(2)}) async-start(f32[8,384,256]{2,1,0:T(8,128)} %broadcast_in_dim.13), calls=%async_computation.2 | async-start | bytes 6291456 | tf_op jit(solution)/shard_map/all_to_all | solution.py:41
  149.1 61.9 %copy-start.1 = (f32[512,448]{0,1:T(8,128)S(1)}, f32[512,448]{0,1:T(8,128)}, u32[]{:S(2)}) copy-start(f32[512,448]{0,1:T(8,128)} %param.5) | copy-start | bytes 2752516
  149.2 61.9 %copy-start.2 = (bf16[512,448]{0,1:T(8,128)(2,1)S(1)}, bf16[512,448]{0,1:T(8,128)(2,1)}, u32[]{:S(2)}) copy-start(bf16[512,448]{0,1:T(8,128)(2,1)} %param.6) | copy-start | bytes 1376260
where the time goes:
time: 278 us; the launch traced here: 277 us
  waiting for transfers between devices  90.6 us (33%)
  blocking collectives  88.7 us (32%)
  other arithmetic  57.7 us (21%)
  starting transfers between devices  16.3 us (6%)
  matrix products  12.1 us (4%)
  local copies, waits for them, and re-layouts  9.05 us (3%)
    all_to_all x2, waiting for transfers between devices, sent_to_all(): lax.all_to_all(jnp.broadcast_to(value[None], (devices, *value.shape)), ax...  90.6 us
    all_to_all x2, blocking collectives, summed_on_arrival(): lax.all_to_all(cut_along(value, dim, devices), axis, 0, 0, tiled=True)  47.5 us
    all_to_all x3, blocking collectives, sent_to_all(): lax.all_to_all(jnp.broadcast_to(value[None], (devices, *value.shape)), ax...  41.2 us
    another operation x7, other arithmetic, orthonormal(): lower_factor = jnp.linalg.cholesky(gram)  34.6 us
    another operation x3, other arithmetic, orthonormal(): jax.scipy.linalg.solve_triangular(lower_factor, row_values.T, lower=True)  19.9 us
    all_to_all x2, starting transfers between devices, sent_to_all(): lax.all_to_all(jnp.broadcast_to(value[None], (devices, *value.shape)), ax...  16.3 us
  transfers between devices with their start and end apart: 2, of which 2 were waited for; matrix products, arithmetic and copies ran while one was open for 0% of the time, Pallas kernels for 0%

commit v1 on v0

v1 whole, which is shorter than its diff:
```python
import functools
import math

import jax
import jax.numpy as jnp
from jax import lax
from jax.experimental import pallas as pl
from jax.experimental.pallas import tpu as pltpu
from jax.sharding import Mesh
from jax.sharding import PartitionSpec as P

ROWS = 4096
COLS = 28672
RANK = 256
SKETCH = 384
Z, X, Y, CORE = "narrow", "wide_0", "wide_1", "wide_2"
WIDE = (X, Y, CORE)
HIGH = lax.Precision.HIGHEST
MESH = pl.DeviceIdType.MESH
BLOCK = 32

decay_mu = 0.95
norm_epsilon = 1e-06


def matmul(a, b):
    return jnp.dot(a, b, precision=HIGH, preferred_element_type=jnp.float32)


def matmul_nt(a, b):
    return lax.dot_general(
        a, b, (((1,), (1,)), ((), ())), precision=HIGH, preferred_element_type=jnp.float32
    )


def matmul_tn(a, b):
    return lax.dot_general(
        a, b, (((0,), (0,)), ((), ())), precision=HIGH, preferred_element_type=jnp.float32
    )


def factor_block(a_ref, inverse_ref, b):
    n = a_ref.shape[0]
    lo, hi = b * BLOCK, (b + 1) * BLOCK
    tile, off = lo // 128, lo % 128
    lane = lax.broadcasted_iota(jnp.int32, (8, 128), 1)
    sub = lax.broadcasted_iota(jnp.int32, (8, 128), 0)
    groups = BLOCK // 8
    rows = [
        a_ref[lo + 8 * q : lo + 8 * q + 8, tile * 128 : (tile + 1) * 128] for q in range(groups)
    ]
    column = {}

    def spread(panel, first):
        for j in range(8 * panel, 8 * panel + 8):
            for q in range(first, groups):
                column[q, j] = jnp.broadcast_to(rows[q][:, off + j : off + j + 1], (8, 128))

    def row_of(value, k):
        return jnp.broadcast_to(value[k : k + 1, :], (8, 128))

    spread(0, 0)
    for p in range(groups):
        if p + 1 < groups:
            spread(p + 1, p)
        for k in range(8):
            kk = 8 * p + k
            here, below = lane == off + kk, sub > k
            root = lax.rsqrt(row_of(column[p, kk], k))
            pivot = jnp.where(here, root, row_of(rows[p], k) * root)
            scaled = {q: column[q, kk] * root for q in range(p, groups)}
            scaled[p] = jnp.where(below, scaled[p], 0.0)
            for j in range(kk + 1, min(8 * (p + 2), BLOCK)):
                share = row_of(column[p, j], k) * root
                for q in range(p, groups):
                    column[q, j] = column[q, j] - scaled[q] * share
            for q in range(p + 1, groups):
                rows[q] = jnp.where(here, 0.0, rows[q]) - scaled[q] * pivot
            rest = jnp.where(here & below, 0.0, rows[p]) - scaled[p] * pivot
            rows[p] = jnp.where(sub == k, pivot, rest)
    corner = jnp.concatenate(
        [
            jnp.where((lane >= off) & (lane <= off + 8 * q + sub), row, 0.0)
            for q, row in enumerate(rows)
        ],
        axis=0,
    )
    solved = matmul(corner, a_ref[tile * 128 : (tile + 1) * 128, :])
    cols = lax.broadcasted_iota(jnp.int32, (BLOCK, n), 1)
    placed = jnp.concatenate(
        [corner if t == tile else jnp.zeros_like(corner) for t in range(n // 128)], axis=1
    )
    solved = jnp.where((cols >= lo) & (cols < hi), placed, solved)
    inverse_ref[lo:hi, :] = jnp.where(cols < hi, solved, 0.0)
    if hi < n:
        start = hi // 128 * 128
        outer = matmul_tn(solved[:, start:], solved)
        cols = lax.broadcasted_iota(jnp.int32, (n - hi, n), 1)
        kept = jnp.where((cols >= lo) & (cols < hi), 0.0, a_ref[hi:n, :])
        a_ref[hi:n, :] = kept - outer[hi - start :, :]


def factors(
    sizes,
    momentum,
    gradient,
    right_basis,
    signs,
    select,
    left_out,
    right_out,
    norm_out,
    summed,
    summed_t,
    part_away,
    part_home,
    core_in,
    chip_sum,
    x_in,
    y_out,
    y_in,
    left_t,
    left_rows,
    parity,
    sketch_out,
    sketch_in,
    sketch_z_out,
    sketch_z,
    sketch_t,
    gram,
    inverse,
    q_out,
    q_in,
    q_all,
    norm_z,
    norm_y,
    norm_x,
    core_sems,
    x_sems,
    y_sems,
    gather_sems,
    sketch_sems,
    q_sems,
    norm_sems,
):
    nz, nx, ny = sizes
    z, x, y, c = (lax.axis_index(name) for name in (Z, X, Y, CORE))
    other = 1 - c
    half = summed.shape[0] // 2
    rank = right_basis.shape[1]

    around = [{CORE: other}]
    around += [{X: lax.rem(x + d, nx)} for d in range(1, nx)]
    around += [{X: lax.rem(x + d, nx), CORE: other} for d in range(1, nx)]
    around += [{Y: lax.rem(y + d, ny)} for d in range(1, ny)]
    around += [{Z: lax.rem(z + d, nz)} for d in range(1, nz)]
    barrier = pltpu.get_barrier_semaphore()
    for device in around:
        pl.semaphore_signal(barrier, inc=1, device_id=device, device_id_type=MESH)

    started = []

    def send(source, target, sems, index, device):
        copy = pltpu.make_async_remote_copy(
            src_ref=source,
            dst_ref=target,
            send_sem=sems.at[0, index],
            recv_sem=sems.at[1, index],
            device_id=device,
            device_id_type=MESH,
        )
        copy.start()
        started.append(copy)
        return copy

    summed[...] = momentum[...] + gradient[...].astype(jnp.float32)
    basis_t = right_basis[...].T
    away = matmul_nt(basis_t, summed[pl.ds(pl.multiple_of(other * half, half), half), :])
    part_away[...] = away.reshape(part_away.shape)
    pl.semaphore_wait(barrier, len(around))
    order = [lax.rem(x + d, nx) for d in range(1, nx)] + [x]
    core_copies = [
        send(part_away.at[to], core_in.at[to], core_sems, i, {CORE: other})
        for i, to in enumerate(order)
    ]
    home = matmul_nt(basis_t, summed[pl.ds(pl.multiple_of(c * half, half), half), :])
    part_home[...] = home.reshape(part_home.shape)

    x_copies = []
    for i, to in enumerate(order):
        core_copies[i].wait_recv()
        total = part_home[to] + core_in[to]
        if i < nx - 1:
            chip_sum[to] = total
            x_copies.append(send(chip_sum.at[to], x_in.at[x], x_sems, i, {X: to}))
        else:
            x_in[x] = total
    place = lax.broadcasted_iota(jnp.int32, parity.shape, 0) + (z * 2 * half + c * half)
    shared = jnp.bitwise_and(place, select[...])
    for shift in (8, 4, 2, 1):
        shared = jnp.bitwise_xor(shared, jnp.right_shift(shared, shift))
    parity[...] = 1.0 - 2.0 * jnp.bitwise_and(shared, 1).astype(jnp.float32)
    for copy in x_copies:
        copy.wait_recv()
    total = x_in[0]
    for i in range(1, nx):
        total = total + x_in[i]
    y_out[...] = total.reshape(y_out.shape)
    y_copies = []
    for d in range(1, ny):
        to = lax.rem(y + d, ny)
        y_copies.append(send(y_out.at[to], y_in.at[y], y_sems, d - 1, {Y: to}))
    y_in[y] = y_out[y]
    summed_t[...] = summed[...].T
    for copy in y_copies:
        copy.wait_recv()
    own = y_in[0]
    for i in range(1, ny):
        own = own + y_in[i]

    mine = x * ny + y

    def along_y(buffer, sems):
        copies = []
        for d in range(1, ny):
            block = buffer.at[c, mine]
            copies.append(send(block, block, sems, d - 1, {Y: lax.rem(y + d, ny)}))
        return copies

    def along_x(buffer, sems, waited):
        for copy in waited:
            copy.wait_recv()
        slab = buffer.at[c, pl.ds(x * ny, ny)]
        copies = []
        for d in range(1, nx):
            copies.append(send(slab, slab, sems, ny - 2 + d, {X: lax.rem(x + d, nx)}))
        return copies, [send(slab, slab, sems, ny + nx - 2, {CORE: other})]

    def along_core(buffer, sems, waited):
        copies = []
        for d, copy in enumerate(waited, 1):
            copy.wait_recv()
            slab = buffer.at[c, pl.ds(lax.rem(x - d + nx, nx) * ny, ny)]
            copies.append(send(slab, slab, sems, ny + nx - 2 + d, {CORE: other}))
        return copies

    left_t[c, mine] = own
    left_y = along_y(left_t, gather_sems.at[0])

    flip = signs[pl.ds(z * 2 + c, 1), :].astype(jnp.float32)
    term = matmul(own * flip, parity[...]) * (1.0 / math.sqrt(SKETCH))
    sketch_out[...] = term
    sketch_copy = send(sketch_out, sketch_in, sketch_sems, 0, {CORE: other})
    sketch_copy.wait_recv()
    term = term + sketch_in[...]
    wide = sketch_z.shape[-1]
    sketch_z_out[0] = term[:, :wide]
    sketch_z_out[1] = term[:, SKETCH - wide :]
    sketch_copies = [
        send(sketch_z_out.at[c], sketch_z.at[z], sketch_sems, d, {Z: lax.rem(z + d, nz)})
        for d in range(1, nz)
    ]
    sketch_z[z] = sketch_z_out[c]

    left_x, left_core = along_x(left_t, gather_sems.at[0], left_y)

    for copy in sketch_copies:
        copy.wait_recv()
    total = sketch_z[0]
    for i in range(1, nz):
        total = total + sketch_z[i]
    sketch_t[c, mine] = total
    sketch_y = along_y(sketch_t, gather_sems.at[1])

    left_core += along_core(left_t, gather_sems.at[0], left_x)
    for copy in left_core:
        copy.wait_recv()

    left_0 = left_t[0].reshape(rank, half)
    left_1 = left_t[1].reshape(rank, half)
    product = matmul_nt(summed_t[:, :half], left_0) + matmul_nt(summed_t[:, half:], left_1)
    q_out[...] = product.reshape(q_out.shape)
    q_copies = []
    for d in range(1, nz):
        to = lax.rem(z + d, nz)
        q_copies.append(send(q_out.at[to], q_in.at[z], q_sems, d - 1, {Z: to}))

    sketch_x, sketch_core = along_x(sketch_t, gather_sems.at[1], sketch_y)
    q_in[z] = q_out[z]
    left_rows[:half, :] = left_0.T
    left_rows[half:, :] = left_1.T
    sketch_core += along_core(sketch_t, gather_sems.at[1], sketch_x)
    for copy in sketch_core:
        copy.wait_recv()

    first = sketch_t[0].reshape(rank, wide)
    last = sketch_t[1].reshape(rank, wide)[:, 2 * wide - SKETCH :]
    gram[...] = matmul_nt(first, first) + matmul_nt(last, last)
    gathered = []
    for b in range(rank // BLOCK):
        factor_block(gram, inverse, b)
        if b == rank // BLOCK // 2:
            for copy in q_copies:
                copy.wait_recv()
            total = q_in[0]
            for i in range(1, nz):
                total = total + q_in[i]
            q_all[z] = total
            for d in range(1, nz):
                block = q_all.at[z]
                to = lax.rem(z + d, nz)
                gathered.append(send(block, block, q_sems, nz - 2 + d, {Z: to}))

    share = matmul_nt(q_all[z], inverse[...])
    norm_z[z] = jnp.sum(share * share, axis=0, keepdims=True)
    copies = [
        send(norm_z.at[z], norm_z.at[z], norm_sems, d, {Z: lax.rem(z + d, nz)})
        for d in range(1, nz)
    ]
    left_out[...] = matmul_nt(left_rows[...], inverse[...])
    for copy in copies:
        copy.wait_recv()
    total = norm_z[0]
    for i in range(1, nz):
        total = total + norm_z[i]
    norm_y[y] = total
    copies = [
        send(norm_y.at[y], norm_y.at[y], norm_sems, nz + d, {Y: lax.rem(y + d, ny)})
        for d in range(1, ny)
    ]
    for copy in copies:
        copy.wait_recv()
    total = norm_y[0]
    for i in range(1, ny):
        total = total + norm_y[i]
    slot = x * 2 + c
    norm_x[slot] = total
    copies = []
    for i, device in enumerate(around[: 2 * nx - 1]):
        copies.append(send(norm_x.at[slot], norm_x.at[slot], norm_sems, nz + ny + i, device))
    for copy in gathered:
        copy.wait_recv()
    right_out[...] = matmul_nt(q_all[...].reshape(right_out.shape), inverse[...])
    for copy in copies:
        copy.wait_recv()
    total = norm_x[0]
    for i in range(1, 2 * nx):
        total = total + norm_x[i]
    norm_out[...] = jnp.sqrt(total + norm_epsilon)
    for copy in started:
        copy.wait_send()


def outputs(
    momentum, gradient, left, right, norms, momentum_out, basis_out, update, basis
):
    @pl.when(pl.program_id(0) == 0)
    def _():
        basis[...] = right[...] / norms[...]
        basis_out[...] = basis[...]

    summed = momentum[...] + gradient[...].astype(jnp.float32)
    momentum_out[...] = summed - (1.0 - decay_mu) * matmul_nt(left[...], right[...])
    update[...] = (math.sqrt(ROWS * COLS / RANK) * matmul_nt(left[...], basis[...])).astype(jnp.bfloat16)


def per_device(sizes, momentum, gradient, right_basis, signs, select):
    nz, nx, ny = sizes
    block_rows, block_cols = momentum.shape
    rank = right_basis.shape[1]
    half = block_rows // 2
    own = rank // (nx * ny)
    wide = 256
    f32 = jnp.float32
    vmem = pl.BlockSpec(memory_space=pltpu.VMEM)
    dma = pltpu.SemaphoreType.DMA
    share = block_cols // nz
    left, right, norms = pl.pallas_call(
        functools.partial(factors, sizes),
        out_shape=(
            jax.ShapeDtypeStruct((block_rows, rank), f32),
            jax.ShapeDtypeStruct((block_cols, rank), f32),
            jax.ShapeDtypeStruct((1, rank), f32),
        ),
        in_specs=[vmem] * 5,
        out_specs=(vmem,) * 3,
        scratch_shapes=[
            pltpu.VMEM((block_rows, block_cols), f32),
            pltpu.VMEM((block_cols, block_rows), f32),
            pltpu.VMEM((nx, rank // nx, half), f32),
            pltpu.VMEM((nx, rank // nx, half), f32),
            pltpu.VMEM((nx, rank // nx, half), f32),
            pltpu.VMEM((nx, rank // nx, half), f32),
            pltpu.VMEM((nx, rank // nx, half), f32),
            pltpu.VMEM((ny, own, half), f32),
            pltpu.VMEM((ny, own, half), f32),
            pltpu.VMEM((2, nx * ny, own, half), f32),
            pltpu.VMEM((block_rows, rank), f32),
            pltpu.VMEM((half, SKETCH), f32),
            pltpu.VMEM((own, SKETCH), f32),
            pltpu.VMEM((own, SKETCH), f32),
            pltpu.VMEM((2, own, wide), f32),
            pltpu.VMEM((nz, own, wide), f32),
            pltpu.VMEM((2, nx * ny, own, wide), f32),
            pltpu.VMEM((rank, rank), f32),
            pltpu.VMEM((rank, rank), f32),
            pltpu.VMEM((nz, share, rank), f32),
            pltpu.VMEM((nz, share, rank), f32),
            pltpu.VMEM((nz, share, rank), f32),
            pltpu.VMEM((nz, 1, rank), f32),
            pltpu.VMEM((ny, 1, rank), f32),
            pltpu.VMEM((2 * nx, 1, rank), f32),
            dma((2, nx)),
            dma((2, nx)),
            dma((2, ny)),
            dma((2, 2, ny + 2 * nx)),
            dma((2, nz)),
            dma((2, 2 * nz)),
            dma((2, nz + ny + 2 * nx)),
        ],
        compiler_params=pltpu.CompilerParams(
            collective_id=0, has_side_effects=True, vmem_limit_bytes=40 << 20
        ),
        name="factors",
    )(
        momentum,
        gradient,
        right_basis,
        signs.reshape(nz * 2, half),
        select.reshape(1, SKETCH),
    )
    rows = min(128, block_rows)
    slab = pl.BlockSpec((rows, block_cols), lambda i: (i, 0))
    whole = pl.BlockSpec((block_cols, rank), lambda i: (0, 0))
    return pl.pallas_call(
        outputs,
        grid=(block_rows // rows,),
        out_shape=(
            jax.ShapeDtypeStruct((block_rows, block_cols), f32),
            jax.ShapeDtypeStruct((block_cols, rank), f32),
            jax.ShapeDtypeStruct((block_rows, block_cols), jnp.bfloat16),
        ),
        in_specs=[
            slab,
            slab,
            pl.BlockSpec((rows, rank), lambda i: (i, 0)),
            whole,
            pl.BlockSpec((1, rank), lambda i: (0, 0)),
        ],
        out_specs=(slab, whole, slab),
        scratch_shapes=[pltpu.VMEM((block_cols, rank), f32)],
        name="outputs",
    )(momentum, gradient, left, right, norms)


def solution(mesh):
    devices = mesh.devices
    shape = (mesh.shape["narrow"], 4, 8, 2) if devices.size == 512 else (2, 2, devices.size // 8, 2)
    split = Mesh(devices.reshape(shape), (Z, X, Y, CORE))
    in_specs = (P(Z, WIDE), P(Z, WIDE), P(WIDE, None), P(), P())
    out_specs = (P(Z, WIDE), P(WIDE, None), P(Z, WIDE))
    return jax.shard_map(
        functools.partial(per_device, shape[:3]),
        mesh=split,
        in_specs=in_specs,
        out_specs=out_specs,
        check_vma=False,
    )
```

time: 278 us -> 95.9 us (0.34)
  waiting for transfers between devices: 90.6 us -> 0 us
  blocking collectives: 88.7 us -> 0 us
  Pallas kernels: 0 us -> 85.4 us
  other arithmetic: 57.7 us -> 0 us
  starting transfers between devices: 16.3 us -> 0 us
  matrix products: 12.1 us -> 0 us
    all_to_all x2 -> x0, waiting for transfers between devices: 90.6 us -> none  [sent_to_all(): lax.all_to_all(jnp.broadcast_to(value[None], (devices, *value.shape)), ax...]
    all_to_all x5 -> x0, blocking collectives: 88.7 us -> none  [the longest x2 47.5 us: summed_on_arrival(): lax.all_to_all(cut_along(value, dim, devices), axis, 0, 0, tiled=True)]
    pallas_call x0 -> x2, Pallas kernels: none -> 85.4 us  [the longest x1 79.4 us: per_device(): pl.pallas_call(functools.partial(factors, sizes), out_shape=(jax.ShapeDty...]
    another operation x10 -> x0, other arithmetic: 54.5 us -> none  [the longest x7 34.6 us: orthonormal(): lower_factor = jnp.linalg.cholesky(gram)]
    all_to_all x2 -> x0, starting transfers between devices: 16.3 us -> none  [sent_to_all(): lax.all_to_all(jnp.broadcast_to(value[None], (devices, *value.shape)), ax...]
    dot_general x6 -> x0, matrix products: 10.4 us -> none  [the longest x1 3.13 us: per_device(): jnp.dot(summed, right_basis, precision=high, preferred_element_type=jnp.f...]
    another operation x9 -> x0, local copies, waits for them, and re-layouts: 4.05 us -> none
    pallas_call x0 -> x2, local copies, waits for them, and re-layouts: none -> 3.48 us  [per_device(): pl.pallas_call(outputs, grid=(block_rows // rows,), out_shape=(jax.ShapeD...]
  transfers between devices with their start and end apart: 2 -> 0, of which waited for: 2 -> 0; matrix products, arithmetic and copies ran while one was open for 0% -> 0% of each run, Pallas kernels for 0% -> 0%
where the time goes in v1:
time: 95.9 us; the launch traced here: 95.6 us
  Pallas kernels  85.4 us (89%)
  local copies, waits for them, and re-layouts  9.53 us (10%)
    pallas_call x1, Pallas kernels, per_device(): pl.pallas_call(functools.partial(factors, sizes), out_shape=(jax.ShapeDty...  79.4 us
    pallas_call x1, Pallas kernels, per_device(): pl.pallas_call(outputs, grid=(block_rows // rows,), out_shape=(jax.ShapeD...  5.96 us
    unnamed x18, local copies, waits for them, and re-layouts  4.56 us
    pallas_call x2, local copies, waits for them, and re-layouts, per_device(): pl.pallas_call(outputs, grid=(block_rows // rows,), out_shape=(jax.ShapeD...  3.48 us

profile of v1, /device:TPU:1, one launch (start us, length us, event | category | flops | bytes accessed | tf_op | source)
XLA Modules:
  0.0 95.6 jit_solution(13990455722505513593)
XLA Ops:
  0.6 0.0 copy-start.6
  0.6 0.8 reshape.13.select
  1.4 0.7 reshape.12.signs
  2.1 1.2 %copy.11.gradient = bf16[512,448]{1,0:T(8,128)(2,1)S(1)} copy(bf16[512,448]{0,1:T(8,128)(2,1)} %param.6) | data formatting | bytes 917504 | tf_op args[1]
  3.4 0.0 copy-done.6
  3.4 0.0 copy-start.1
  3.4 0.0 copy-start.4
  3.4 0.3 copy.10.momentum
  3.7 0.4 copy-done.1
  4.2 0.4 copy-done.4
  4.6 0.0 copy-start
  4.6 79.4 %factors.1 = (f32[512,256]{1,0:T(8,128)S(1)}, f32[448,256]{1,0:T(8,128)S(1)}, f32[1,256]{1,0:T(1,128)S(1)}) custom-call(f32[512,448]{1,0:T(8,128)S(1)} %copy.10.momentum, bf16[512,448]{1,0:T(8,128)(2,1)S(1)} %copy.11.gradient, f32[448,256]{1,0:T(8,128)S(1)} %copy-done.4, s32[16,256]{1,0:T(8,128)S(1)} %reshape.12.signs, s32[1,384]{1,0:T(1,128)S(1)} %reshape.13.select), custom_call_target="tpu_custom_call" | custom-call | tf_op jit(solution)/shard_map/factors/pallas_call | solution.py:378
  84.0 0.0 copy-start.2
  84.0 0.8 copy-done.2
  84.8 0.0 copy-start.3
  84.8 0.8 copy-done.3
  85.6 0.0 copy-start.5
  85.6 0.6 copy-done.5
  86.1 0.0 copy-done
  86.1 6.0 %outputs.1 = (f32[512,448]{1,0:T(8,128)}, f32[448,256]{1,0:T(8,128)}, bf16[512,448]{1,0:T(8,128)(2,1)}) custom-call(f32[512,448]{1,0:T(8,128)} %copy-done, bf16[512,448]{1,0:T(8,128)(2,1)} %copy-done.1, f32[512,256]{1,0:T(8,128)} %copy-done.2, f32[448,256]{1,0:T(8,128)} %copy-done.3, f32[1,256]{1,0:T(1,128)} %copy-done.5), custom_call_target="tpu_custom_call" | custom-call | tf_op jit(solution)/shard_map/outputs/pallas_call | solution.py:435
  92.1 0.0 copy-start.7
  92.1 2.5 %copy.12 = f32[512,448]{0,1:T(8,128)} copy(f32[512,448]{1,0:T(8,128)} %get-tuple-element.9) | data formatting | bytes 1835008 | tf_op jit(solution)/shard_map/outputs/pallas_call | solution.py:435
  94.6 0.0 copy-done.7
  94.6 1.0 %copy.13 = bf16[512,448]{0,1:T(8,128)(2,1)} copy(bf16[512,448]{1,0:T(8,128)(2,1)S(1)} %copy-done.7) | data formatting | bytes 917504 | tf_op jit(solution)/shard_map/outputs/pallas_call | solution.py:435
Async XLA Ops:
  0.6 2.7 %copy-start.6 = (f32[512,448]{0,1:T(8,128)S(1)}, f32[512,448]{0,1:T(8,128)}, u32[]{:S(2)}) copy-start(f32[512,448]{0,1:T(8,128)} %param.5) | copy-start | bytes 2752516
  3.4 0.8 copy-start.1
  3.4 1.2 %copy-start.4 = (f32[448,256]{1,0:T(8,128)S(1)}, f32[448,256]{1,0:T(8,128)}, u32[]{:S(2)}) copy-start(f32[448,256]{1,0:T(8,128)} %right_basis.1) | copy-start | bytes 1376260
  4.6 81.6 %copy-start = (f32[512,448]{1,0:T(8,128)}, f32[512,448]{1,0:T(8,128)S(1)}, u32[]{:S(2)}) copy-start(f32[512,448]{1,0:T(8,128)S(1)} %copy.10.momentum) | copy-start | bytes 2752516
  84.0 0.8 copy-start.2
  84.8 0.8 copy-start.3
  85.6 0.6 copy-start.5
  92.1 2.5 %copy-start.7 = (bf16[512,448]{1,0:T(8,128)(2,1)S(1)}, bf16[512,448]{1,0:T(8,128)(2,1)}, u32[]{:S(2)}) copy-start(bf16[512,448]{1,0:T(8,128)(2,1)} %get-tuple-element.11) | copy-start | bytes 1376260

commit v2 on v1

--- a/solution.py
+++ b/solution.py
@@ -102,16 +102,24 @@
 
 def factors(
     sizes,
+    momentum_in,
+    gradient_in,
+    basis_in,
+    signs_in,
+    select_in,
+    left_out,
+    right_out,
+    norm_out,
+    summed_out,
+    summed_t,
+    left,
+    right,
+    norms,
     momentum,
     gradient,
     right_basis,
     signs,
     select,
-    left_out,
-    right_out,
-    norm_out,
-    summed,
-    summed_t,
     part_away,
     part_home,
     core_in,
@@ -120,7 +128,6 @@
     y_out,
     y_in,
     left_t,
-    left_rows,
     parity,
     sketch_out,
     sketch_in,
@@ -132,26 +139,41 @@
     q_out,
     q_in,
     q_all,
-    norm_z,
-    norm_y,
-    norm_x,
+    norm_near,
+    norm_far,
     core_sems,
     x_sems,
     y_sems,
     gather_sems,
     sketch_sems,
     q_sems,
-    norm_sems,
+    near_sems,
+    far_sems,
+    load_sems,
+    store_sems,
 ):
     nz, nx, ny = sizes
     z, x, y, c = (lax.axis_index(name) for name in (Z, X, Y, CORE))
     other = 1 - c
-    half = summed.shape[0] // 2
+    half = summed_t.shape[1] // 2
+    loads = [
+        pltpu.make_async_copy(source, target, load_sems.at[i])
+        for i, (source, target) in enumerate(
+            (
+                (momentum_in, momentum),
+                (gradient_in, gradient),
+                (basis_in, right_basis),
+                (signs_in, signs),
+                (select_in, select),
+            )
+        )
+    ]
+    for load in loads:
+        load.start()
     rank = right_basis.shape[1]
 
     around = [{CORE: other}]
     around += [{X: lax.rem(x + d, nx)} for d in range(1, nx)]
-    around += [{X: lax.rem(x + d, nx), CORE: other} for d in range(1, nx)]
     around += [{Y: lax.rem(y + d, ny)} for d in range(1, ny)]
     around += [{Z: lax.rem(z + d, nz)} for d in range(1, nz)]
     barrier = pltpu.get_barrier_semaphore()
@@ -159,6 +181,12 @@
         pl.semaphore_signal(barrier, inc=1, device_id=device, device_id_type=MESH)
 
     started = []
+    stores = []
+
+    def store(source, target):
+        copy = pltpu.make_async_copy(source, target, store_sems.at[len(stores)])
+        copy.start()
+        stores.append(copy)
 
     def send(source, target, sems, index, device):
         copy = pltpu.make_async_remote_copy(
@@ -173,9 +201,11 @@
         started.append(copy)
         return copy
 
-    summed[...] = momentum[...] + gradient[...].astype(jnp.float32)
+    for load in loads:
+        load.wait()
+    summed_t[...] = momentum[...] + gradient[...].astype(jnp.float32)
     basis_t = right_basis[...].T
-    away = matmul_nt(basis_t, summed[pl.ds(pl.multiple_of(other * half, half), half), :])
+    away = matmul(basis_t, summed_t[:, pl.ds(pl.multiple_of(other * half, half), half)])
     part_away[...] = away.reshape(part_away.shape)
     pl.semaphore_wait(barrier, len(around))
     order = [lax.rem(x + d, nx) for d in range(1, nx)] + [x]
@@ -183,7 +213,8 @@
         send(part_away.at[to], core_in.at[to], core_sems, i, {CORE: other})
         for i, to in enumerate(order)
     ]
-    home = matmul_nt(basis_t, summed[pl.ds(pl.multiple_of(c * half, half), half), :])
+    store(summed_t, summed_out)
+    home = matmul(basis_t, summed_t[:, pl.ds(pl.multiple_of(c * half, half), half)])
     part_home[...] = home.reshape(part_home.shape)
 
     x_copies = []
@@ -196,7 +227,7 @@
         else:
             x_in[x] = total
     place = lax.broadcasted_iota(jnp.int32, parity.shape, 0) + (z * 2 * half + c * half)
-    shared = jnp.bitwise_and(place, select[...])
+    shared = jnp.bitwise_and(place, select[...].reshape(1, SKETCH))
     for shift in (8, 4, 2, 1):
         shared = jnp.bitwise_xor(shared, jnp.right_shift(shared, shift))
     parity[...] = 1.0 - 2.0 * jnp.bitwise_and(shared, 1).astype(jnp.float32)
@@ -211,7 +242,6 @@
         to = lax.rem(y + d, ny)
         y_copies.append(send(y_out.at[to], y_in.at[y], y_sems, d - 1, {Y: to}))
     y_in[y] = y_out[y]
-    summed_t[...] = summed[...].T
     for copy in y_copies:
         copy.wait_recv()
     own = y_in[0]
@@ -247,7 +277,7 @@
     left_t[c, mine] = own
     left_y = along_y(left_t, gather_sems.at[0])
 
-    flip = signs[pl.ds(z * 2 + c, 1), :].astype(jnp.float32)
+    flip = signs[pl.ds(pl.multiple_of((z * 2 + c) * half, half), half)].reshape(1, half).astype(jnp.float32)
     term = matmul(own * flip, parity[...]) * (1.0 / math.sqrt(SKETCH))
     sketch_out[...] = term
     sketch_copy = send(sketch_out, sketch_in, sketch_sems, 0, {CORE: other})
@@ -287,8 +317,6 @@
 
     sketch_x, sketch_core = along_x(sketch_t, gather_sems.at[1], sketch_y)
     q_in[z] = q_out[z]
-    left_rows[:half, :] = left_0.T
-    left_rows[half:, :] = left_1.T
     sketch_core += along_core(sketch_t, gather_sems.at[1], sketch_x)
     for copy in sketch_core:
         copy.wait_recv()
@@ -299,7 +327,7 @@
     gathered = []
     for b in range(rank // BLOCK):
         factor_block(gram, inverse, b)
-        if b == rank // BLOCK // 2:
+        if b == 2:
             for copy in q_copies:
                 copy.wait_recv()
             total = q_in[0]
@@ -312,81 +340,136 @@
                 gathered.append(send(block, block, q_sems, nz - 2 + d, {Z: to}))
 
     share = matmul_nt(q_all[z], inverse[...])
-    norm_z[z] = jnp.sum(share * share, axis=0, keepdims=True)
-    copies = [
-        send(norm_z.at[z], norm_z.at[z], norm_sems, d, {Z: lax.rem(z + d, nz)})
-        for d in range(1, nz)
-    ]
-    left_out[...] = matmul_nt(left_rows[...], inverse[...])
-    for copy in copies:
-        copy.wait_recv()
-    total = norm_z[0]
-    for i in range(1, nz):
-        total = total + norm_z[i]
-    norm_y[y] = total
-    copies = [
-        send(norm_y.at[y], norm_y.at[y], norm_sems, nz + d, {Y: lax.rem(y + d, ny)})
-        for d in range(1, ny)
-    ]
-    for copy in copies:
-        copy.wait_recv()
-    total = norm_y[0]
-    for i in range(1, ny):
-        total = total + norm_y[i]
-    slot = x * 2 + c
-    norm_x[slot] = total
-    copies = []
-    for i, device in enumerate(around[: 2 * nx - 1]):
-        copies.append(send(norm_x.at[slot], norm_x.at[slot], norm_sems, nz + ny + i, device))
+    slot = y * 2 + c
+    norm_near[slot] = jnp.sum(share * share, axis=0, keepdims=True)
+    near = []
+    for d in range(1, 2 * ny):
+        device = {Y: lax.rem(y + d // 2, ny), CORE: lax.rem(c + d, 2)}
+        near.append(send(norm_near.at[slot], norm_near.at[slot], near_sems, d, device))
+    left[:, :half] = matmul(inverse[...], left_0)
+    left[:, half:] = matmul(inverse[...], left_1)
+    store(left, left_out)
+    for copy in near:
+        copy.wait_recv()
+    total = norm_near[0]
+    for i in range(1, 2 * ny):
+        total = total + norm_near[i]
+    slot = z * nx + x
+    norm_far[slot] = total
+    far = []
+    for d in range(1, nz * nx):
+        device = {Z: lax.rem(z + d // nx, nz), X: lax.rem(x + d, nx)}
+        far.append(send(norm_far.at[slot], norm_far.at[slot], far_sems, d, device))
     for copy in gathered:
         copy.wait_recv()
-    right_out[...] = matmul_nt(q_all[...].reshape(right_out.shape), inverse[...])
-    for copy in copies:
-        copy.wait_recv()
-    total = norm_x[0]
-    for i in range(1, 2 * nx):
-        total = total + norm_x[i]
-    norm_out[...] = jnp.sqrt(total + norm_epsilon)
+    right[...] = matmul_nt(q_all[...].reshape(right.shape), inverse[...])
+    store(right, right_out)
+    for copy in far:
+        copy.wait_recv()
+    total = norm_far[0]
+    for i in range(1, nz * nx):
+        total = total + norm_far[i]
+    norms[...] = jnp.sqrt(total + norm_epsilon)
+    store(norms, norm_out)
     for copy in started:
         copy.wait_send()
+    for copy in stores:
+        copy.wait()
+
+
+def split(value):
+    high = value.astype(jnp.bfloat16)
+    return high, (value - high.astype(jnp.float32)).astype(jnp.bfloat16)
 
 
 def outputs(
-    momentum, gradient, left, right, norms, momentum_out, basis_out, update, basis
+    summed_in,
+    left_in,
+    right_in,
+    norms_in,
+    moved_out,
+    basis_out,
+    update_out,
+    summed,
+    left,
+    right,
+    norms,
+    moved,
+    basis,
+    update,
+    load_sems,
+    sems,
+    *,
+    steps,
 ):
-    @pl.when(pl.program_id(0) == 0)
-    def _():
-        basis[...] = right[...] / norms[...]
-        basis_out[...] = basis[...]
-
-    summed = momentum[...] + gradient[...].astype(jnp.float32)
-    momentum_out[...] = summed - (1.0 - decay_mu) * matmul_nt(left[...], right[...])
-    update[...] = (math.sqrt(ROWS * COLS / RANK) * matmul_nt(left[...], basis[...])).astype(jnp.bfloat16)
+    columns, rank = right.shape
+    step = columns // steps
+    loads = [
+        pltpu.make_async_copy(source, target, load_sems.at[i])
+        for i, (source, target) in enumerate(
+            ((left_in, left), (right_in, right), (norms_in, norms), (summed_in, summed))
+        )
+    ]
+    for load in loads:
+        load.start()
+    loads[0].wait()
+    left_high, left_low = split(left[...])
+    loads[1].wait()
+    loads[2].wait()
+    basis[...] = right[...] / norms[...]
+    copies = [pltpu.make_async_copy(basis, basis_out, sems.at[0])]
+    copies[0].start()
+    for i in range(steps):
+        rows = pl.ds(i * step, step)
+        both = jnp.concatenate([right[rows, :], basis[rows, :]], axis=0)
+        high, low = split(both)
+        product = jnp.dot(high, left_low, preferred_element_type=jnp.float32)
+        product += jnp.dot(low, left_high, preferred_element_type=jnp.float32)
+        product += jnp.dot(high, left_high, preferred_element_type=jnp.float32)
+        if i == 0:
+            loads[3].wait()
+        moved[rows, :] = summed[rows, :] - (1.0 - decay_mu) * product[:step]
+        update[rows, :] = (math.sqrt(ROWS * COLS / RANK) * product[step:]).astype(jnp.bfloat16)
+        for k, (source, target) in enumerate(((moved, moved_out), (update, update_out))):
+            copy = pltpu.make_async_copy(source.at[rows], target.at[rows], sems.at[1 + 2 * i + k])
+            copy.start()
+            copies.append(copy)
+    for copy in copies:
+        copy.wait()
 
 
 def per_device(sizes, momentum, gradient, right_basis, signs, select):
     nz, nx, ny = sizes
-    block_rows, block_cols = momentum.shape
+    momentum, gradient = momentum.T, gradient.T
+    block_cols, block_rows = momentum.shape
     rank = right_basis.shape[1]
     half = block_rows // 2
     own = rank // (nx * ny)
     wide = 256
     f32 = jnp.float32
-    vmem = pl.BlockSpec(memory_space=pltpu.VMEM)
+    hbm = pl.BlockSpec(memory_space=pltpu.HBM)
     dma = pltpu.SemaphoreType.DMA
     share = block_cols // nz
-    left, right, norms = pl.pallas_call(
+    left, right, norms, summed = pl.pallas_call(
         functools.partial(factors, sizes),
         out_shape=(
-            jax.ShapeDtypeStruct((block_rows, rank), f32),
+            jax.ShapeDtypeStruct((rank, block_rows), f32),
             jax.ShapeDtypeStruct((block_cols, rank), f32),
             jax.ShapeDtypeStruct((1, rank), f32),
+            jax.ShapeDtypeStruct((block_cols, block_rows), f32),
         ),
-        in_specs=[vmem] * 5,
-        out_specs=(vmem,) * 3,
+        in_specs=[hbm] * 5,
+        out_specs=(hbm,) * 4,
         scratch_shapes=[
-            pltpu.VMEM((block_rows, block_cols), f32),
             pltpu.VMEM((block_cols, block_rows), f32),
+            pltpu.VMEM((rank, block_rows), f32),
+            pltpu.VMEM((block_cols, rank), f32),
+            pltpu.VMEM((1, rank), f32),
+            pltpu.VMEM((block_cols, block_rows), f32),
+            pltpu.VMEM((block_cols, block_rows), jnp.bfloat16),
+            pltpu.VMEM((block_cols, rank), f32),
+            pltpu.VMEM((ROWS,), jnp.int32),
+            pltpu.VMEM((SKETCH,), jnp.int32),
             pltpu.VMEM((nx, rank // nx, half), f32),
             pltpu.VMEM((nx, rank // nx, half), f32),
             pltpu.VMEM((nx, rank // nx, half), f32),
@@ -395,7 +478,6 @@
             pltpu.VMEM((ny, own, half), f32),
             pltpu.VMEM((ny, own, half), f32),
             pltpu.VMEM((2, nx * ny, own, half), f32),
-            pltpu.VMEM((block_rows, rank), f32),
             pltpu.VMEM((half, SKETCH), f32),
             pltpu.VMEM((own, SKETCH), f32),
             pltpu.VMEM((own, SKETCH), f32),
@@ -407,50 +489,55 @@
             pltpu.VMEM((nz, share, rank), f32),
             pltpu.VMEM((nz, share, rank), f32),
             pltpu.VMEM((nz, share, rank), f32),
-            pltpu.VMEM((nz, 1, rank), f32),
-            pltpu.VMEM((ny, 1, rank), f32),
-            pltpu.VMEM((2 * nx, 1, rank), f32),
+            pltpu.VMEM((2 * ny, 1, rank), f32),
+            pltpu.VMEM((nz * nx, 1, rank), f32),
             dma((2, nx)),
             dma((2, nx)),
             dma((2, ny)),
             dma((2, 2, ny + 2 * nx)),
             dma((2, nz)),
             dma((2, 2 * nz)),
-            dma((2, nz + ny + 2 * nx)),
+            dma((2, 2 * ny)),
+            dma((2, nz * nx)),
+            dma((5,)),
+            dma((4,)),
         ],
         compiler_params=pltpu.CompilerParams(
-            collective_id=0, has_side_effects=True, vmem_limit_bytes=40 << 20
+            collective_id=0, has_side_effects=True, vmem_limit_bytes=64000 << 10
         ),
         name="factors",
     )(
         momentum,
         gradient,
         right_basis,
-        signs.reshape(nz * 2, half),
-        select.reshape(1, SKETCH),
+        signs,
+        select,
     )
-    rows = min(128, block_rows)
-    slab = pl.BlockSpec((rows, block_cols), lambda i: (i, 0))
-    whole = pl.BlockSpec((block_cols, rank), lambda i: (0, 0))
-    return pl.pallas_call(
-        outputs,
-        grid=(block_rows // rows,),
+    steps = 4
+    moved, basis, update = pl.pallas_call(
+        functools.partial(outputs, steps=steps),
         out_shape=(
-            jax.ShapeDtypeStruct((block_rows, block_cols), f32),
+            jax.ShapeDtypeStruct((block_cols, block_rows), f32),
             jax.ShapeDtypeStruct((block_cols, rank), f32),
-            jax.ShapeDtypeStruct((block_rows, block_cols), jnp.bfloat16),
+            jax.ShapeDtypeStruct((block_cols, block_rows), jnp.bfloat16),
         ),
-        in_specs=[
-            slab,
-            slab,
-            pl.BlockSpec((rows, rank), lambda i: (i, 0)),
-            whole,
-            pl.BlockSpec((1, rank), lambda i: (0, 0)),
+        in_specs=[hbm] * 4,
+        out_specs=(hbm,) * 3,
+        scratch_shapes=[
+            pltpu.VMEM((block_cols, block_rows), f32),
+            pltpu.VMEM((rank, block_rows), f32),
+            pltpu.VMEM((block_cols, rank), f32),
+            pltpu.VMEM((1, rank), f32),
+            pltpu.VMEM((block_cols, block_rows), f32),
+            pltpu.VMEM((block_cols, rank), f32),
+            pltpu.VMEM((block_cols, block_rows), jnp.bfloat16),
+            dma((4,)),
+            dma((1 + 2 * steps,)),
         ],
-        out_specs=(slab, whole, slab),
-        scratch_shapes=[pltpu.VMEM((block_cols, rank), f32)],
+        compiler_params=pltpu.CompilerParams(vmem_limit_bytes=64000 << 10),
         name="outputs",
-    )(momentum, gradient, left, right, norms)
+    )(summed, left, right, norms)
+    return moved.T, basis, update.T
 
 
 def solution(mesh):

time: 95.9 us -> 77.8 us (0.81)
  local copies, waits for them, and re-layouts: 9.53 us -> 0 us
  Pallas kernels: 85.4 us -> 77 us
    pallas_call x1, Pallas kernels: 79.4 us -> 73.9 us  [per_device(): pl.pallas_call(functools.partial(factors, sizes), out_shape=(jax.ShapeDty...]
    unnamed x18 -> x0, local copies, waits for them, and re-layouts: 4.56 us -> none
    pallas_call x2 -> x0, local copies, waits for them, and re-layouts: 3.48 us -> none  [per_device(): pl.pallas_call(outputs, grid=(block_rows // rows,), out_shape=(jax.ShapeD...]
    pallas_call x1, Pallas kernels: 5.96 us -> 3.04 us  [per_device(): pl.pallas_call(functools.partial(outputs, steps=steps), out_shape=(jax.Sh...]
    reshape x2 -> x0, local copies, waits for them, and re-layouts: 1.49 us -> none  [the longest x1 0.76 us: per_device(): select.reshape(1, SKETCH)]
where the time goes in v2:
time: 77.8 us; the launch traced here: 77.6 us
  Pallas kernels  77 us (99%)
    pallas_call x1, Pallas kernels, per_device(): pl.pallas_call(functools.partial(factors, sizes), out_shape=(jax.ShapeDty...  73.9 us
    pallas_call x1, Pallas kernels, per_device(): pl.pallas_call(functools.partial(outputs, steps=steps), out_shape=(jax.Sh...  3.04 us

profile of v2, /device:TPU:1, one launch (start us, length us, event | category | flops | bytes accessed | tf_op | source)
XLA Modules:
  0.0 77.6 jit_solution(12836893529905606992)
XLA Ops:
  0.6 73.9 %factors.1 = (f32[256,512]{1,0:T(8,128)}, f32[448,256]{1,0:T(8,128)}, f32[1,256]{1,0:T(1,128)}, f32[448,512]{1,0:T(8,128)}) custom-call(f32[448,512]{1,0:T(8,128)} %bitcast.4, bf16[448,512]{1,0:T(8,128)(2,1)} %bitcast.5, f32[448,256]{1,0:T(8,128)} %basis_in.1, s32[4096]{0:T(1024)} %signs_in.1, s32[384]{0:T(512)} %select_in.1), custom_call_target="tpu_custom_call" | custom-call | tf_op jit(solution)/shard_map/factors/pallas_call | solution.py:453
  74.6 3.0 %outputs.1 = (f32[448,512]{1,0:T(8,128)}, f32[448,256]{1,0:T(8,128)}, bf16[448,512]{1,0:T(8,128)(2,1)}) custom-call(f32[448,512]{1,0:T(8,128)} %get-tuple-element.10.summed_in, f32[256,512]{1,0:T(8,128)} %get-tuple-element.11.left_in, f32[448,256]{1,0:T(8,128)} %get-tuple-element.12.right_in, f32[1,256]{1,0:T(1,128)} %get-tuple-element.13.norms_in), custom_call_target="tpu_custom_call" | custom-call | tf_op jit(solution)/shard_map/outputs/pallas_call | solution.py:517

commit v3 on v2

--- a/solution.py
+++ b/solution.py
@@ -17,7 +17,7 @@
 WIDE = (X, Y, CORE)
 HIGH = lax.Precision.HIGHEST
 MESH = pl.DeviceIdType.MESH
-BLOCK = 32
+BLOCK = 64
 
 decay_mu = 0.95
 norm_epsilon = 1e-06
@@ -62,7 +62,7 @@
     spread(0, 0)
     for p in range(groups):
         if p + 1 < groups:
-            spread(p + 1, p)
+            spread(p + 1, p + 1)
         for k in range(8):
             kk = 8 * p + k
             here, below = lane == off + kk, sub > k
@@ -71,8 +71,8 @@
             scaled = {q: column[q, kk] * root for q in range(p, groups)}
             scaled[p] = jnp.where(below, scaled[p], 0.0)
             for j in range(kk + 1, min(8 * (p + 2), BLOCK)):
-                share = row_of(column[p, j], k) * root
-                for q in range(p, groups):
+                share = row_of(scaled[j // 8], j % 8)
+                for q in range(j // 8, groups):
                     column[q, j] = column[q, j] - scaled[q] * share
             for q in range(p + 1, groups):
                 rows[q] = jnp.where(here, 0.0, rows[q]) - scaled[q] * pivot
@@ -258,20 +258,26 @@
         return copies
 
     def along_x(buffer, sems, waited):
-        for copy in waited:
-            copy.wait_recv()
-        slab = buffer.at[c, pl.ds(x * ny, ny)]
+        copies = []
+        for i, k in enumerate([0] + [k for d in range(1, ny // 2 + 1) for k in (d, ny - d)][: ny - 1]):
+            if k:
+                waited[k - 1].wait_recv()
+            block = buffer.at[c, x * ny + lax.rem(y - k + ny, ny)]
+            for d in range(1, nx):
+                device = {X: lax.rem(x + d, nx)}
+                copies.append(send(block, block, sems, ny - 1 + i * nx + d, device))
+            if k == ny // 2:
+                slab = buffer.at[c, pl.ds(x * ny, ny)]
+                last = [send(slab, slab, sems, ny - 1 + i * nx, {CORE: other})]
+        return copies, last
+
+    def along_core(buffer, sems, waited):
         copies = []
         for d in range(1, nx):
-            copies.append(send(slab, slab, sems, ny - 2 + d, {X: lax.rem(x + d, nx)}))
-        return copies, [send(slab, slab, sems, ny + nx - 2, {CORE: other})]
-
-    def along_core(buffer, sems, waited):
-        copies = []
-        for d, copy in enumerate(waited, 1):
-            copy.wait_recv()
+            for copy in waited[d - 1 :: nx - 1]:
+                copy.wait_recv()
             slab = buffer.at[c, pl.ds(lax.rem(x - d + nx, nx) * ny, ny)]
-            copies.append(send(slab, slab, sems, ny + nx - 2 + d, {CORE: other}))
+            copies.append(send(slab, slab, sems, ny - 1 + ny * nx + d, {CORE: other}))
         return copies
 
     left_t[c, mine] = own
@@ -327,7 +333,7 @@
     gathered = []
     for b in range(rank // BLOCK):
         factor_block(gram, inverse, b)
-        if b == 2:
+        if b == rank // BLOCK // 2 - 1:
             for copy in q_copies:
                 copy.wait_recv()
             total = q_in[0]
@@ -494,7 +500,7 @@
             dma((2, nx)),
             dma((2, nx)),
             dma((2, ny)),
-            dma((2, 2, ny + 2 * nx)),
+            dma((2, 2, ny + (ny + 1) * nx)),
             dma((2, nz)),
             dma((2, 2 * nz)),
             dma((2, 2 * ny)),

time: 77.8 us -> 75.7 us (0.973)
  Pallas kernels: 77 us -> 74.8 us
    pallas_call x1, Pallas kernels: 73.9 us -> 71.7 us  [per_device(): pl.pallas_call(functools.partial(factors, sizes), out_shape=(jax.ShapeDty...]
where the time goes in v3:
time: 75.7 us; the launch traced here: 75.6 us
  Pallas kernels  74.8 us (99%)
  between operations  0.8 us (1%)
    pallas_call x1, Pallas kernels, per_device(): pl.pallas_call(functools.partial(factors, sizes), out_shape=(jax.ShapeDty...  71.7 us
    pallas_call x1, Pallas kernels, per_device(): pl.pallas_call(functools.partial(outputs, steps=steps), out_shape=(jax.Sh...  3.04 us

profile of v3, /device:TPU:1, one launch (start us, length us, event | category | flops | bytes accessed | tf_op | source)
XLA Modules:
  0.0 75.6 jit_solution(8951755262615058494)
XLA Ops:
  0.6 71.7 %factors.1 = (f32[256,512]{1,0:T(8,128)}, f32[448,256]{1,0:T(8,128)}, f32[1,256]{1,0:T(1,128)}, f32[448,512]{1,0:T(8,128)}) custom-call(f32[448,512]{1,0:T(8,128)} %bitcast.4, bf16[448,512]{1,0:T(8,128)(2,1)} %bitcast.5, f32[448,256]{1,0:T(8,128)} %basis_in.1, s32[4096]{0:T(1024)} %signs_in.1, s32[384]{0:T(512)} %select_in.1), custom_call_target="tpu_custom_call" | custom-call | tf_op jit(solution)/shard_map/factors/pallas_call | solution.py:459
  72.3 3.0 %outputs.1 = (f32[448,512]{1,0:T(8,128)}, f32[448,256]{1,0:T(8,128)}, bf16[448,512]{1,0:T(8,128)(2,1)}) custom-call(f32[448,512]{1,0:T(8,128)} %get-tuple-element.10.summed_in, f32[256,512]{1,0:T(8,128)} %get-tuple-element.11.left_in, f32[448,256]{1,0:T(8,128)} %get-tuple-element.12.right_in, f32[1,256]{1,0:T(1,128)} %get-tuple-element.13.norms_in), custom_call_target="tpu_custom_call" | custom-call | tf_op jit(solution)/shard_map/outputs/pallas_call | solution.py:523

commit v4 on v3

--- a/solution.py
+++ b/solution.py
@@ -110,11 +110,8 @@
     left_out,
     right_out,
     norm_out,
-    summed_out,
     summed_t,
-    left,
-    right,
-    norms,
+    basis_t,
     momentum,
     gradient,
     right_basis,
@@ -128,12 +125,12 @@
     y_out,
     y_in,
     left_t,
+    left_full,
     parity,
-    sketch_out,
-    sketch_in,
     sketch_z_out,
     sketch_z,
     sketch_t,
+    sketch_full,
     gram,
     inverse,
     q_out,
@@ -150,7 +147,6 @@
     near_sems,
     far_sems,
     load_sems,
-    store_sems,
 ):
     nz, nx, ny = sizes
     z, x, y, c = (lax.axis_index(name) for name in (Z, X, Y, CORE))
@@ -181,12 +177,6 @@
         pl.semaphore_signal(barrier, inc=1, device_id=device, device_id_type=MESH)
 
     started = []
-    stores = []
-
-    def store(source, target):
-        copy = pltpu.make_async_copy(source, target, store_sems.at[len(stores)])
-        copy.start()
-        stores.append(copy)
 
     def send(source, target, sems, index, device):
         copy = pltpu.make_async_remote_copy(
@@ -204,17 +194,17 @@
     for load in loads:
         load.wait()
     summed_t[...] = momentum[...] + gradient[...].astype(jnp.float32)
-    basis_t = right_basis[...].T
-    away = matmul(basis_t, summed_t[:, pl.ds(pl.multiple_of(other * half, half), half)])
+    basis_t[...] = right_basis[...].T
+    rows = rank // 2
+    away = matmul(basis_t[pl.ds(pl.multiple_of(other * rows, rows), rows), :], summed_t[...])
     part_away[...] = away.reshape(part_away.shape)
     pl.semaphore_wait(barrier, len(around))
-    order = [lax.rem(x + d, nx) for d in range(1, nx)] + [x]
+    order = [lax.rem(x + d, nx) for d in sorted(range(1, nx), key=lambda d: -min(d, nx - d))] + [x]
     core_copies = [
         send(part_away.at[to], core_in.at[to], core_sems, i, {CORE: other})
         for i, to in enumerate(order)
     ]
-    store(summed_t, summed_out)
-    home = matmul(basis_t, summed_t[:, pl.ds(pl.multiple_of(c * half, half), half)])
+    home = matmul(basis_t[pl.ds(pl.multiple_of(c * rows, rows), rows), :], summed_t[...])
     part_home[...] = home.reshape(part_home.shape)
 
     x_copies = []
@@ -226,7 +216,7 @@
             x_copies.append(send(chip_sum.at[to], x_in.at[x], x_sems, i, {X: to}))
         else:
             x_in[x] = total
-    place = lax.broadcasted_iota(jnp.int32, parity.shape, 0) + (z * 2 * half + c * half)
+    place = lax.broadcasted_iota(jnp.int32, parity.shape, 0) + z * 2 * half
     shared = jnp.bitwise_and(place, select[...].reshape(1, SKETCH))
     for shift in (8, 4, 2, 1):
         shared = jnp.bitwise_xor(shared, jnp.right_shift(shared, shift))
@@ -236,7 +226,10 @@
     total = x_in[0]
     for i in range(1, nx):
         total = total + x_in[i]
-    y_out[...] = total.reshape(y_out.shape)
+    own_rows = total.shape[0] // ny
+    for i in range(ny):
+        part = total[i * own_rows : (i + 1) * own_rows]
+        y_out[i] = jnp.concatenate([part[:, :half], part[:, half:]], axis=0)
     y_copies = []
     for d in range(1, ny):
         to = lax.rem(y + d, ny)
@@ -280,23 +273,32 @@
             copies.append(send(slab, slab, sems, ny - 1 + ny * nx + d, {CORE: other}))
         return copies
 
+    def unpacked(buffer):
+        pieces = []
+        for core in range(2):
+            for i in range(0, nx * ny, 2):
+                a, b = buffer[core, i], buffer[core, i + 1]
+                start = core * rows + i * own_rows
+                low = jnp.concatenate([a[:own_rows], b[:own_rows]], axis=0)
+                high = jnp.concatenate([a[own_rows:], b[own_rows:]], axis=0)
+                pieces.append((slice(start, start + 2 * own_rows), low, high))
+        return pieces
+
     left_t[c, mine] = own
     left_y = along_y(left_t, gather_sems.at[0])
 
-    flip = signs[pl.ds(pl.multiple_of((z * 2 + c) * half, half), half)].reshape(1, half).astype(jnp.float32)
-    term = matmul(own * flip, parity[...]) * (1.0 / math.sqrt(SKETCH))
-    sketch_out[...] = term
-    sketch_copy = send(sketch_out, sketch_in, sketch_sems, 0, {CORE: other})
-    sketch_copy.wait_recv()
-    term = term + sketch_in[...]
+    flip = signs[pl.ds(pl.multiple_of(z * 2 * half, 2 * half), 2 * half)]
+    flip = flip.reshape(1, 2 * half).astype(jnp.float32)
+    low = matmul(own * flip[:, :half], parity[:half, :])
+    high = matmul(own * flip[:, half:], parity[half:, :])
+    term = (low[:own_rows] + high[own_rows:]) * (1.0 / math.sqrt(SKETCH))
     wide = sketch_z.shape[-1]
-    sketch_z_out[0] = term[:, :wide]
-    sketch_z_out[1] = term[:, SKETCH - wide :]
+    sketch_z_out[...] = jnp.concatenate([term[:, :wide], term[:, SKETCH - wide :]], axis=0)
     sketch_copies = [
-        send(sketch_z_out.at[c], sketch_z.at[z], sketch_sems, d, {Z: lax.rem(z + d, nz)})
+        send(sketch_z_out, sketch_z.at[z], sketch_sems, d, {Z: lax.rem(z + d, nz)})
         for d in range(1, nz)
     ]
-    sketch_z[z] = sketch_z_out[c]
+    sketch_z[z] = sketch_z_out[...]
 
     left_x, left_core = along_x(left_t, gather_sems.at[0], left_y)
 
@@ -312,9 +314,10 @@
     for copy in left_core:
         copy.wait_recv()
 
-    left_0 = left_t[0].reshape(rank, half)
-    left_1 = left_t[1].reshape(rank, half)
-    product = matmul_nt(summed_t[:, :half], left_0) + matmul_nt(summed_t[:, half:], left_1)
+    for top, low, high in unpacked(left_t):
+        left_full[top, :half] = low
+        left_full[top, half:] = high
+    product = matmul_nt(summed_t[...], left_full[...])
     q_out[...] = product.reshape(q_out.shape)
     q_copies = []
     for d in range(1, nz):
@@ -327,13 +330,14 @@
     for copy in sketch_core:
         copy.wait_recv()
 
-    first = sketch_t[0].reshape(rank, wide)
-    last = sketch_t[1].reshape(rank, wide)[:, 2 * wide - SKETCH :]
-    gram[...] = matmul_nt(first, first) + matmul_nt(last, last)
+    for top, low, high in unpacked(sketch_t):
+        sketch_full[top, :wide] = low
+        sketch_full[top, wide:] = high[:, 2 * wide - SKETCH :]
+    gram[...] = matmul_nt(sketch_full[...], sketch_full[...])
     gathered = []
     for b in range(rank // BLOCK):
         factor_block(gram, inverse, b)
-        if b == rank // BLOCK // 2 - 1:
+        if b == 0:
             for copy in q_copies:
                 copy.wait_recv()
             total = q_in[0]
@@ -352,9 +356,7 @@
     for d in range(1, 2 * ny):
         device = {Y: lax.rem(y + d // 2, ny), CORE: lax.rem(c + d, 2)}
         near.append(send(norm_near.at[slot], norm_near.at[slot], near_sems, d, device))
-    left[:, :half] = matmul(inverse[...], left_0)
-    left[:, half:] = matmul(inverse[...], left_1)
-    store(left, left_out)
+    left_out[...] = matmul(inverse[...], left_full[...])
     for copy in near:
         copy.wait_recv()
     total = norm_near[0]
@@ -368,19 +370,15 @@
         far.append(send(norm_far.at[slot], norm_far.at[slot], far_sems, d, device))
     for copy in gathered:
         copy.wait_recv()
-    right[...] = matmul_nt(q_all[...].reshape(right.shape), inverse[...])
-    store(right, right_out)
+    right_out[...] = matmul_nt(q_all[...].reshape(right_out.shape), inverse[...])
     for copy in far:
         copy.wait_recv()
     total = norm_far[0]
     for i in range(1, nz * nx):
         total = total + norm_far[i]
-    norms[...] = jnp.sqrt(total + norm_epsilon)
-    store(norms, norm_out)
+    norm_out[...] = jnp.sqrt(total + norm_epsilon)
     for copy in started:
         copy.wait_send()
-    for copy in stores:
-        copy.wait()
 
 
 def split(value):
@@ -389,39 +387,23 @@
 
 
 def outputs(
-    summed_in,
-    left_in,
-    right_in,
-    norms_in,
-    moved_out,
-    basis_out,
-    update_out,
     summed,
     left,
     right,
     norms,
+    moved_out,
+    basis_out,
+    update_out,
     moved,
     basis,
     update,
-    load_sems,
     sems,
     *,
     steps,
 ):
     columns, rank = right.shape
     step = columns // steps
-    loads = [
-        pltpu.make_async_copy(source, target, load_sems.at[i])
-        for i, (source, target) in enumerate(
-            ((left_in, left), (right_in, right), (norms_in, norms), (summed_in, summed))
-        )
-    ]
-    for load in loads:
-        load.start()
-    loads[0].wait()
     left_high, left_low = split(left[...])
-    loads[1].wait()
-    loads[2].wait()
     basis[...] = right[...] / norms[...]
     copies = [pltpu.make_async_copy(basis, basis_out, sems.at[0])]
     copies[0].start()
@@ -432,8 +414,6 @@
         product = jnp.dot(high, left_low, preferred_element_type=jnp.float32)
         product += jnp.dot(low, left_high, preferred_element_type=jnp.float32)
         product += jnp.dot(high, left_high, preferred_element_type=jnp.float32)
-        if i == 0:
-            loads[3].wait()
         moved[rows, :] = summed[rows, :] - (1.0 - decay_mu) * product[:step]
         update[rows, :] = (math.sqrt(ROWS * COLS / RANK) * product[step:]).astype(jnp.bfloat16)
         for k, (source, target) in enumerate(((moved, moved_out), (update, update_out))):
@@ -446,13 +426,17 @@
 
 def per_device(sizes, momentum, gradient, right_basis, signs, select):
     nz, nx, ny = sizes
-    momentum, gradient = momentum.T, gradient.T
+    momentum, gradient, right_basis, signs, select = (
+        pltpu.with_memory_space_constraint(value, pltpu.HBM)
+        for value in (momentum.T, gradient.T, right_basis, signs, select)
+    )
     block_cols, block_rows = momentum.shape
     rank = right_basis.shape[1]
     half = block_rows // 2
-    own = rank // (nx * ny)
+    own = 2 * rank // (2 * nx * ny)
     wide = 256
     f32 = jnp.float32
+    vmem = pl.BlockSpec(memory_space=pltpu.VMEM)
     hbm = pl.BlockSpec(memory_space=pltpu.HBM)
     dma = pltpu.SemaphoreType.DMA
     share = block_cols // nz
@@ -465,31 +449,28 @@
             jax.ShapeDtypeStruct((block_cols, block_rows), f32),
         ),
         in_specs=[hbm] * 5,
-        out_specs=(hbm,) * 4,
+        out_specs=(vmem,) * 4,
         scratch_shapes=[
-            pltpu.VMEM((block_cols, block_rows), f32),
-            pltpu.VMEM((rank, block_rows), f32),
-            pltpu.VMEM((block_cols, rank), f32),
-            pltpu.VMEM((1, rank), f32),
+            pltpu.VMEM((rank, block_cols), f32),
             pltpu.VMEM((block_cols, block_rows), f32),
             pltpu.VMEM((block_cols, block_rows), jnp.bfloat16),
             pltpu.VMEM((block_cols, rank), f32),
             pltpu.VMEM((ROWS,), jnp.int32),
             pltpu.VMEM((SKETCH,), jnp.int32),
-            pltpu.VMEM((nx, rank // nx, half), f32),
-            pltpu.VMEM((nx, rank // nx, half), f32),
-            pltpu.VMEM((nx, rank // nx, half), f32),
-            pltpu.VMEM((nx, rank // nx, half), f32),
-            pltpu.VMEM((nx, rank // nx, half), f32),
+            pltpu.VMEM((nx, rank // (2 * nx), block_rows), f32),
+            pltpu.VMEM((nx, rank // (2 * nx), block_rows), f32),
+            pltpu.VMEM((nx, rank // (2 * nx), block_rows), f32),
+            pltpu.VMEM((nx, rank // (2 * nx), block_rows), f32),
+            pltpu.VMEM((nx, rank // (2 * nx), block_rows), f32),
             pltpu.VMEM((ny, own, half), f32),
             pltpu.VMEM((ny, own, half), f32),
             pltpu.VMEM((2, nx * ny, own, half), f32),
-            pltpu.VMEM((half, SKETCH), f32),
-            pltpu.VMEM((own, SKETCH), f32),
-            pltpu.VMEM((own, SKETCH), f32),
-            pltpu.VMEM((2, own, wide), f32),
+            pltpu.VMEM((rank, block_rows), f32),
+            pltpu.VMEM((block_rows, SKETCH), f32),
+            pltpu.VMEM((own, wide), f32),
             pltpu.VMEM((nz, own, wide), f32),
             pltpu.VMEM((2, nx * ny, own, wide), f32),
+            pltpu.VMEM((rank, SKETCH), f32),
             pltpu.VMEM((rank, rank), f32),
             pltpu.VMEM((rank, rank), f32),
             pltpu.VMEM((nz, share, rank), f32),
@@ -506,10 +487,9 @@
             dma((2, 2 * ny)),
             dma((2, nz * nx)),
             dma((5,)),
-            dma((4,)),
         ],
         compiler_params=pltpu.CompilerParams(
-            collective_id=0, has_side_effects=True, vmem_limit_bytes=64000 << 10
+            collective_id=0, has_side_effects=True, vmem_limit_bytes=40 << 20
         ),
         name="factors",
     )(
@@ -527,20 +507,15 @@
             jax.ShapeDtypeStruct((block_cols, rank), f32),
             jax.ShapeDtypeStruct((block_cols, block_rows), jnp.bfloat16),
         ),
-        in_specs=[hbm] * 4,
+        in_specs=[vmem] * 4,
         out_specs=(hbm,) * 3,
         scratch_shapes=[
             pltpu.VMEM((block_cols, block_rows), f32),
-            pltpu.VMEM((rank, block_rows), f32),
-            pltpu.VMEM((block_cols, rank), f32),
-            pltpu.VMEM((1, rank), f32),
-            pltpu.VMEM((block_cols, block_rows), f32),
             pltpu.VMEM((block_cols, rank), f32),
             pltpu.VMEM((block_cols, block_rows), jnp.bfloat16),
-            dma((4,)),
             dma((1 + 2 * steps,)),
         ],
-        compiler_params=pltpu.CompilerParams(vmem_limit_bytes=64000 << 10),
+        compiler_params=pltpu.CompilerParams(vmem_limit_bytes=20 << 20),
         name="outputs",
     )(summed, left, right, norms)
     return moved.T, basis, update.T

time: 75.7 us -> 76.1 us (level)
    pallas_call x1, Pallas kernels: 71.7 us -> 73.4 us  [per_device(): pl.pallas_call(functools.partial(factors, sizes), out_shape=(jax.ShapeDty...]
    pallas_call x1, Pallas kernels: 3.04 us -> 1.72 us  [per_device(): pl.pallas_call(functools.partial(outputs, steps=steps), out_shape=(jax.Sh...]
where the time goes in v4:
time: 76.1 us; the launch traced here: 75.9 us
  Pallas kernels  75.1 us (99%)
  between operations  0.8 us (1%)
    pallas_call x1, Pallas kernels, per_device(): pl.pallas_call(functools.partial(factors, sizes), out_shape=(jax.ShapeDty...  73.4 us
    pallas_call x1, Pallas kernels, per_device(): pl.pallas_call(functools.partial(outputs, steps=steps), out_shape=(jax.Sh...  1.72 us

profile of v4, /device:TPU:1, one launch (start us, length us, event | category | flops | bytes accessed | tf_op | source)
XLA Modules:
  0.0 75.9 jit_solution(4843633337234337328)
XLA Ops:
  0.6 73.4 %factors.1 = (f32[256,512]{1,0:T(8,128)S(1)}, f32[448,256]{1,0:T(8,128)S(1)}, f32[1,256]{1,0:T(1,128)S(1)}, f32[448,512]{1,0:T(8,128)S(1)}) custom-call(f32[448,512]{1,0:T(8,128)} %bitcast.4, bf16[448,512]{1,0:T(8,128)(2,1)} %bitcast.5, f32[448,256]{1,0:T(8,128)} %basis_in.1, s32[4096]{0:T(1024)} %signs_in.1, s32[384]{0:T(512)} %select_in.1), custom_call_target="tpu_custom_call" | custom-call | tf_op jit(solution)/shard_map/factors/pallas_call | solution.py:443
  74.0 1.7 %outputs.1 = (f32[448,512]{1,0:T(8,128)}, f32[448,256]{1,0:T(8,128)}, bf16[448,512]{1,0:T(8,128)(2,1)}) custom-call(f32[448,512]{1,0:T(8,128)S(1)} %get-tuple-element.10.summed, f32[256,512]{1,0:T(8,128)S(1)} %get-tuple-element.11.left, f32[448,256]{1,0:T(8,128)S(1)} %get-tuple-element.12.right, f32[1,256]{1,0:T(1,128)S(1)} %get-tuple-element.13.norms), custom_call_target="tpu_custom_call" | custom-call | tf_op jit(solution)/shard_map/outputs/pallas_call | solution.py:503

commit v5 on v4

--- a/solution.py
+++ b/solution.py
@@ -37,6 +37,17 @@
     return lax.dot_general(
         a, b, (((0,), (0,)), ((), ())), precision=HIGH, preferred_element_type=jnp.float32
     )
+
+
+def sign_product(value, signs):
+    rows = value.shape[0]
+    pieces = []
+    for _ in range(3):
+        pieces.append(value.astype(jnp.bfloat16).astype(jnp.float32))
+        value = value - pieces[-1]
+    stacked = jnp.concatenate(pieces, axis=0).astype(jnp.bfloat16)
+    product = jnp.dot(stacked, signs, preferred_element_type=jnp.float32)
+    return product[:rows] + product[rows : 2 * rows] + product[2 * rows :]
 
 
 def factor_block(a_ref, inverse_ref, b):
@@ -135,6 +146,7 @@
     inverse,
     q_out,
     q_in,
+    q_relay,
     q_all,
     norm_near,
     norm_far,
@@ -220,7 +232,7 @@
     shared = jnp.bitwise_and(place, select[...].reshape(1, SKETCH))
     for shift in (8, 4, 2, 1):
         shared = jnp.bitwise_xor(shared, jnp.right_shift(shared, shift))
-    parity[...] = 1.0 - 2.0 * jnp.bitwise_and(shared, 1).astype(jnp.float32)
+    parity[...] = (1.0 - 2.0 * jnp.bitwise_and(shared, 1).astype(jnp.float32)).astype(jnp.bfloat16)
     for copy in x_copies:
         copy.wait_recv()
     total = x_in[0]
@@ -289,8 +301,8 @@
 
     flip = signs[pl.ds(pl.multiple_of(z * 2 * half, 2 * half), 2 * half)]
     flip = flip.reshape(1, 2 * half).astype(jnp.float32)
-    low = matmul(own * flip[:, :half], parity[:half, :])
-    high = matmul(own * flip[:, half:], parity[half:, :])
+    low = sign_product(own * flip[:, :half], parity[:half, :])
+    high = sign_product(own * flip[:, half:], parity[half:, :])
     term = (low[:own_rows] + high[own_rows:]) * (1.0 / math.sqrt(SKETCH))
     wide = sketch_z.shape[-1]
     sketch_z_out[...] = jnp.concatenate([term[:, :wide], term[:, SKETCH - wide :]], axis=0)
@@ -319,13 +331,29 @@
         left_full[top, half:] = high
     product = matmul_nt(summed_t[...], left_full[...])
     q_out[...] = product.reshape(q_out.shape)
-    q_copies = []
-    for d in range(1, nz):
-        to = lax.rem(z + d, nz)
-        q_copies.append(send(q_out.at[to], q_in.at[z], q_sems, d - 1, {Z: to}))
+    at = [lax.rem(z + d, nz) for d in range(nz)]
+    cut = q_out.shape[1] // 16 * 8 + 8
+    upper, lower = pl.ds(0, cut), pl.ds(cut, q_out.shape[1] - cut)
+    relayed = [
+        send(q_out.at[at[4], upper], q_in.at[5, upper], q_sems, 5, {Z: at[2]}),
+        send(q_out.at[at[4], lower], q_in.at[7, lower], q_sems, 7, {Z: at[6]}),
+        send(q_out.at[at[3]], q_in.at[4], q_sems, 4, {Z: at[1]}),
+        send(q_out.at[at[5]], q_in.at[6], q_sems, 6, {Z: at[7]}),
+    ]
+    q_copies = [
+        send(q_out.at[at[1]], q_in.at[0], q_sems, 0, {Z: at[1]}),
+        send(q_out.at[at[7]], q_in.at[1], q_sems, 1, {Z: at[7]}),
+    ]
 
     sketch_x, sketch_core = along_x(sketch_t, gather_sems.at[1], sketch_y)
-    q_in[z] = q_out[z]
+    for copy in relayed:
+        copy.wait_recv()
+    q_relay[0] = q_out[at[2]] + q_in[4]
+    q_relay[0, upper] += q_in[5, upper]
+    q_relay[1] = q_out[at[6]] + q_in[6]
+    q_relay[1, lower] += q_in[7, lower]
+    q_copies.append(send(q_relay.at[0], q_in.at[2], q_sems, 2, {Z: at[2]}))
+    q_copies.append(send(q_relay.at[1], q_in.at[3], q_sems, 3, {Z: at[6]}))
     sketch_core += along_core(sketch_t, gather_sems.at[1], sketch_x)
     for copy in sketch_core:
         copy.wait_recv()
@@ -337,17 +365,13 @@
     gathered = []
     for b in range(rank // BLOCK):
         factor_block(gram, inverse, b)
-        if b == 0:
+        if b == 1:
             for copy in q_copies:
                 copy.wait_recv()
-            total = q_in[0]
-            for i in range(1, nz):
-                total = total + q_in[i]
-            q_all[z] = total
-            for d in range(1, nz):
+            q_all[z] = q_out[z] + q_in[0] + q_in[1] + q_in[2] + q_in[3]
+            for k, d in enumerate((2, 6, 1, 7)):
                 block = q_all.at[z]
-                to = lax.rem(z + d, nz)
-                gathered.append(send(block, block, q_sems, nz - 2 + d, {Z: to}))
+                gathered.append(send(block, block, q_sems, nz + k, {Z: at[d]}))
 
     share = matmul_nt(q_all[z], inverse[...])
     slot = y * 2 + c
@@ -357,6 +381,17 @@
         device = {Y: lax.rem(y + d // 2, ny), CORE: lax.rem(c + d, 2)}
         near.append(send(norm_near.at[slot], norm_near.at[slot], near_sems, d, device))
     left_out[...] = matmul(inverse[...], left_full[...])
+    for copy in gathered[:2]:
+        copy.wait_recv()
+    passed = [
+        (q_all.at[at[6], upper], at[2]),
+        (q_all.at[at[2], lower], at[6]),
+        (q_all.at[at[6]], at[1]),
+        (q_all.at[at[2]], at[7]),
+    ]
+    gathered = gathered[2:] + [
+        send(block, block, q_sems, nz + 4 + k, {Z: to}) for k, (block, to) in enumerate(passed)
+    ]
     for copy in near:
         copy.wait_recv()
     total = norm_near[0]
@@ -466,7 +501,7 @@
             pltpu.VMEM((ny, own, half), f32),
             pltpu.VMEM((2, nx * ny, own, half), f32),
             pltpu.VMEM((rank, block_rows), f32),
-            pltpu.VMEM((block_rows, SKETCH), f32),
+            pltpu.VMEM((block_rows, SKETCH), jnp.bfloat16),
             pltpu.VMEM((own, wide), f32),
             pltpu.VMEM((nz, own, wide), f32),
             pltpu.VMEM((2, nx * ny, own, wide), f32),
@@ -475,6 +510,7 @@
             pltpu.VMEM((rank, rank), f32),
             pltpu.VMEM((nz, share, rank), f32),
             pltpu.VMEM((nz, share, rank), f32),
+            pltpu.VMEM((2, share, rank), f32),
             pltpu.VMEM((nz, share, rank), f32),
             pltpu.VMEM((2 * ny, 1, rank), f32),
             pltpu.VMEM((nz * nx, 1, rank), f32),

time: 76.1 us -> 71.1 us (0.934)
  Pallas kernels: 75.1 us -> 70.1 us
    pallas_call x1, Pallas kernels: 73.4 us -> 68.4 us  [per_device(): pl.pallas_call(functools.partial(factors, sizes), out_shape=(jax.ShapeDty...]
where the time goes in v5:
time: 71.1 us; the launch traced here: 70.9 us
  Pallas kernels  70.1 us (99%)
  between operations  0.8 us (1%)
    pallas_call x1, Pallas kernels, per_device(): pl.pallas_call(functools.partial(factors, sizes), out_shape=(jax.ShapeDty...  68.4 us
    pallas_call x1, Pallas kernels, per_device(): pl.pallas_call(functools.partial(outputs, steps=steps), out_shape=(jax.Sh...  1.72 us

profile of v5, /device:TPU:1, one launch (start us, length us, event | category | flops | bytes accessed | tf_op | source)
XLA Modules:
  0.0 70.9 jit_solution(12926125477548427374)
XLA Ops:
  0.6 68.4 %factors.1 = (f32[256,512]{1,0:T(8,128)S(1)}, f32[448,256]{1,0:T(8,128)S(1)}, f32[1,256]{1,0:T(1,128)S(1)}, f32[448,512]{1,0:T(8,128)S(1)}) custom-call(f32[448,512]{1,0:T(8,128)} %bitcast.4, bf16[448,512]{1,0:T(8,128)(2,1)} %bitcast.5, f32[448,256]{1,0:T(8,128)} %basis_in.1, s32[4096]{0:T(1024)} %signs_in.1, s32[384]{0:T(512)} %select_in.1), custom_call_target="tpu_custom_call" | custom-call | tf_op jit(solution)/shard_map/factors/pallas_call | solution.py:478
  69.0 1.7 %outputs.1 = (f32[448,512]{1,0:T(8,128)}, f32[448,256]{1,0:T(8,128)}, bf16[448,512]{1,0:T(8,128)(2,1)}) custom-call(f32[448,512]{1,0:T(8,128)S(1)} %get-tuple-element.10.summed, f32[256,512]{1,0:T(8,128)S(1)} %get-tuple-element.11.left, f32[448,256]{1,0:T(8,128)S(1)} %get-tuple-element.12.right, f32[1,256]{1,0:T(1,128)S(1)} %get-tuple-element.13.norms), custom_call_target="tpu_custom_call" | custom-call | tf_op jit(solution)/shard_map/outputs/pallas_call | solution.py:539

commit v6 on v5

--- a/solution.py
+++ b/solution.py
@@ -37,6 +37,10 @@
     return lax.dot_general(
         a, b, (((0,), (0,)), ((), ())), precision=HIGH, preferred_element_type=jnp.float32
     )
+
+
+def far_first(size):
+    return sorted(range(1, size), key=lambda d: -min(d, size - d))
 
 
 def sign_product(value, signs):
@@ -211,7 +215,7 @@
     away = matmul(basis_t[pl.ds(pl.multiple_of(other * rows, rows), rows), :], summed_t[...])
     part_away[...] = away.reshape(part_away.shape)
     pl.semaphore_wait(barrier, len(around))
-    order = [lax.rem(x + d, nx) for d in sorted(range(1, nx), key=lambda d: -min(d, nx - d))] + [x]
+    order = [lax.rem(x + d, nx) for d in far_first(nx)] + [x]
     core_copies = [
         send(part_away.at[to], core_in.at[to], core_sems, i, {CORE: other})
         for i, to in enumerate(order)
@@ -243,7 +247,7 @@
         part = total[i * own_rows : (i + 1) * own_rows]
         y_out[i] = jnp.concatenate([part[:, :half], part[:, half:]], axis=0)
     y_copies = []
-    for d in range(1, ny):
+    for d in far_first(ny):
         to = lax.rem(y + d, ny)
         y_copies.append(send(y_out.at[to], y_in.at[y], y_sems, d - 1, {Y: to}))
     y_in[y] = y_out[y]
@@ -256,21 +260,21 @@
     mine = x * ny + y
 
     def along_y(buffer, sems):
-        copies = []
-        for d in range(1, ny):
+        copies = {}
+        for d in far_first(ny):
             block = buffer.at[c, mine]
-            copies.append(send(block, block, sems, d - 1, {Y: lax.rem(y + d, ny)}))
+            copies[d] = send(block, block, sems, d - 1, {Y: lax.rem(y + d, ny)})
         return copies
 
     def along_x(buffer, sems, waited):
-        copies = []
+        copies = {d: [] for d in range(1, nx)}
         for i, k in enumerate([0] + [k for d in range(1, ny // 2 + 1) for k in (d, ny - d)][: ny - 1]):
             if k:
-                waited[k - 1].wait_recv()
+                waited[k].wait_recv()
             block = buffer.at[c, x * ny + lax.rem(y - k + ny, ny)]
-            for d in range(1, nx):
+            for d in far_first(nx):
                 device = {X: lax.rem(x + d, nx)}
-                copies.append(send(block, block, sems, ny - 1 + i * nx + d, device))
+                copies[d].append(send(block, block, sems, ny - 1 + i * nx + d, device))
             if k == ny // 2:
                 slab = buffer.at[c, pl.ds(x * ny, ny)]
                 last = [send(slab, slab, sems, ny - 1 + i * nx, {CORE: other})]
@@ -278,8 +282,8 @@
 
     def along_core(buffer, sems, waited):
         copies = []
-        for d in range(1, nx):
-            for copy in waited[d - 1 :: nx - 1]:
+        for d in reversed(far_first(nx)):
+            for copy in waited[d]:
                 copy.wait_recv()
             slab = buffer.at[c, pl.ds(lax.rem(x - d + nx, nx) * ny, ny)]
             copies.append(send(slab, slab, sems, ny - 1 + ny * nx + d, {CORE: other}))
@@ -308,7 +312,7 @@
     sketch_z_out[...] = jnp.concatenate([term[:, :wide], term[:, SKETCH - wide :]], axis=0)
     sketch_copies = [
         send(sketch_z_out, sketch_z.at[z], sketch_sems, d, {Z: lax.rem(z + d, nz)})
-        for d in range(1, nz)
+        for d in far_first(nz)
     ]
     sketch_z[z] = sketch_z_out[...]
 
@@ -346,6 +350,7 @@
     ]
 
     sketch_x, sketch_core = along_x(sketch_t, gather_sems.at[1], sketch_y)
+    sketch_core += along_core(sketch_t, gather_sems.at[1], sketch_x)
     for copy in relayed:
         copy.wait_recv()
     q_relay[0] = q_out[at[2]] + q_in[4]
@@ -354,7 +359,6 @@
     q_relay[1, lower] += q_in[7, lower]
     q_copies.append(send(q_relay.at[0], q_in.at[2], q_sems, 2, {Z: at[2]}))
     q_copies.append(send(q_relay.at[1], q_in.at[3], q_sems, 3, {Z: at[6]}))
-    sketch_core += along_core(sketch_t, gather_sems.at[1], sketch_x)
     for copy in sketch_core:
         copy.wait_recv()
 
@@ -377,7 +381,7 @@
     slot = y * 2 + c
     norm_near[slot] = jnp.sum(share * share, axis=0, keepdims=True)
     near = []
-    for d in range(1, 2 * ny):
+    for d in sorted(range(1, 2 * ny), key=lambda d: -min(d // 2, ny - d // 2)):
         device = {Y: lax.rem(y + d // 2, ny), CORE: lax.rem(c + d, 2)}
         near.append(send(norm_near.at[slot], norm_near.at[slot], near_sems, d, device))
     left_out[...] = matmul(inverse[...], left_full[...])
@@ -400,7 +404,10 @@
     slot = z * nx + x
     norm_far[slot] = total
     far = []
-    for d in range(1, nz * nx):
+    for d in sorted(
+        range(1, nz * nx),
+        key=lambda d: -min(d // nx, nz - d // nx) - min(d % nx, nx - d % nx),
+    ):
         device = {Z: lax.rem(z + d // nx, nz), X: lax.rem(x + d, nx)}
         far.append(send(norm_far.at[slot], norm_far.at[slot], far_sems, d, device))
     for copy in gathered:

time: 71.1 us -> 68.9 us (0.969)
  Pallas kernels: 70.1 us -> 68 us
    pallas_call x1, Pallas kernels: 68.4 us -> 66.2 us  [per_device(): pl.pallas_call(functools.partial(factors, sizes), out_shape=(jax.ShapeDty...]
where the time goes in v6:
time: 68.9 us; the launch traced here: 68.8 us
  Pallas kernels  68 us (99%)
  between operations  0.8 us (1%)
    pallas_call x1, Pallas kernels, per_device(): pl.pallas_call(functools.partial(factors, sizes), out_shape=(jax.ShapeDty...  66.2 us
    pallas_call x1, Pallas kernels, per_device(): pl.pallas_call(functools.partial(outputs, steps=steps), out_shape=(jax.Sh...  1.72 us

profile of v6, /device:TPU:1, one launch (start us, length us, event | category | flops | bytes accessed | tf_op | source)
XLA Modules:
  0.0 68.8 jit_solution(14359177960782785410)
XLA Ops:
  0.6 66.2 %factors.1 = (f32[256,512]{1,0:T(8,128)S(1)}, f32[448,256]{1,0:T(8,128)S(1)}, f32[1,256]{1,0:T(1,128)S(1)}, f32[448,512]{1,0:T(8,128)S(1)}) custom-call(f32[448,512]{1,0:T(8,128)} %bitcast.4, bf16[448,512]{1,0:T(8,128)(2,1)} %bitcast.5, f32[448,256]{1,0:T(8,128)} %basis_in.1, s32[4096]{0:T(1024)} %signs_in.1, s32[384]{0:T(512)} %select_in.1), custom_call_target="tpu_custom_call" | custom-call | tf_op jit(solution)/shard_map/factors/pallas_call | solution.py:485
  66.9 1.7 %outputs.1 = (f32[448,512]{1,0:T(8,128)}, f32[448,256]{1,0:T(8,128)}, bf16[448,512]{1,0:T(8,128)(2,1)}) custom-call(f32[448,512]{1,0:T(8,128)S(1)} %get-tuple-element.10.summed, f32[256,512]{1,0:T(8,128)S(1)} %get-tuple-element.11.left, f32[448,256]{1,0:T(8,128)S(1)} %get-tuple-element.12.right, f32[1,256]{1,0:T(1,128)S(1)} %get-tuple-element.13.norms), custom_call_target="tpu_custom_call" | custom-call | tf_op jit(solution)/shard_map/outputs/pallas_call | solution.py:546
